TPU v7x, 32 devices: a whole 2x2x4 slice. The times are simulated.
32 devices in a mesh: row: 4 (over z), head: 8 (over y, x, core).
Axes of the slice: x: 2, y: 2, z: 4, core: 2. Of those that a mesh axis runs over, the one named last changes fastest.
Arguments:
- q_nope: bfloat16 [512, 16384], P('row', 'head'), may hold values from -6 to 6
- q_rope: bfloat16 [512, 8192], P('row', 'head'), may hold values from -192 to 192
- latent_keys: bfloat16 [512, 1024], P(None, 'row'), may hold values from -6 to 6
- rope_keys: bfloat16 [64, 1024], P(None, 'row'), may hold values from -8 to 8
- panel_block: int32 [4], replicated, may hold values from 0 to 15, as said below
- query_pos: int32 [512], P('row'), may hold values from 1 to 4095
- w_uk: bfloat16 [128, 128, 512], P('head'), may hold values from -0.5 to 0.5
- w_uv: bfloat16 [128, 512, 128], P('head'), may hold values from -1 to 1
- w_out: bfloat16 [7168, 16384], P('row', 'head'), may hold values from -0.09375 to 0.09375
Outputs:
- attn_out: bfloat16 [512, 7168], P(('row', 'head'))
Inputs may be any that keep to these rules, and one draw needn't show every extreme that they name: `panel_block`: distinct block numbers; 0 and the largest allowed block are always among them.
All inputs are finite; a program needn't handle non-finite values.
Results may differ from a plain program's by a relative error of at most 0.025.
Values may be sent and summed in bfloat16 or wider, within the bound.
No kernel may reach another device: no remote copies, remote signals or barrier semaphores. Data moves between devices by JAX's collectives and lax.ppermute only.
A program may use at most 64 MiB of HBM per device.

v0:
```python
import functools

import jax
import jax.numpy as jnp
from jax import lax
from jax.experimental import pallas as pl
from jax.experimental.pallas import tpu as pltpu
from jax.sharding import PartitionSpec as P


NOPE = 128
ROPE = 64
LATENT = 512
VHEAD = 128
PANEL = 256


softmax_scale = 192.0 ** (-0.5)


def in_hbm(x):
    return pltpu.with_memory_space_constraint(x, pltpu.HBM)


def swap(x, axis, mask):
    count = lax.axis_size(axis)
    return lax.ppermute(x, axis, [(i, i ^ mask) for i in range(count)])


def gather_blocks(own):
    count = lax.axis_size("row")
    blocks = {0: own}
    mask = count // 2
    while mask:
        for k in list(blocks):
            moved = []
            for chunk in blocks[k]:
                moved.append(swap(chunk, "row", mask))
            blocks[k ^ mask] = moved
        mask //= 2
    return [blocks[k] for k in range(count)]


def half_kernel(latent_ref, rope_ref, out_ref, sems):
    half = out_ref.shape[1]
    side = lax.axis_index("head") & 1
    columns = pl.ds(pl.multiple_of(side * half, half), half)
    latent = pltpu.make_async_copy(latent_ref.at[:, columns], out_ref.at[:LATENT], sems.at[0])
    rope = pltpu.make_async_copy(rope_ref.at[:, columns], out_ref.at[LATENT:], sems.at[1])
    latent.start()
    rope.start()
    latent.wait()
    rope.wait()


def panel_half(latent_keys, rope_keys):
    half = latent_keys.shape[1] // 2
    depth = LATENT + ROPE
    whole = pl.BlockSpec(memory_space=pltpu.HBM)
    return pl.pallas_call(
        half_kernel,
        in_specs=[whole, whole],
        out_specs=pl.BlockSpec(memory_space=pltpu.VMEM),
        out_shape=jax.ShapeDtypeStruct((depth, half), jnp.bfloat16),
        scratch_shapes=[pltpu.SemaphoreType.DMA((2,))],
        compiler_params=pltpu.CompilerParams(vmem_limit_bytes=2 * 1024 * 1024),
        cost_estimate=pl.CostEstimate(flops=1000000, bytes_accessed=4 * depth * half, transcendentals=0),
        name="panel_half",
    )(in_hbm(latent_keys), in_hbm(rope_keys))


def load_kernel(hbm_ref, out_ref, sem):
    copy = pltpu.make_async_copy(hbm_ref, out_ref, sem)
    copy.start()
    copy.wait()


def load(x):
    return pl.pallas_call(
        load_kernel,
        in_specs=[pl.BlockSpec(memory_space=pltpu.HBM)],
        out_specs=pl.BlockSpec(memory_space=pltpu.VMEM),
        out_shape=pltpu.VMEM(x.shape, x.dtype),
        scratch_shapes=[pltpu.SemaphoreType.DMA],
        compiler_params=pltpu.CompilerParams(vmem_limit_bytes=1024 * 1024 + 2 * x.size),
        cost_estimate=pl.CostEstimate(flops=4000000, bytes_accessed=2 * x.size, transcendentals=0),
        name="load",
    )(in_hbm(x))


def query_kernel(heads, nope_ref, absorb_ref, out_ref):
    for h in range(heads):
        out_ref[h] = jnp.dot(
            nope_ref[:, h * NOPE : (h + 1) * NOPE], absorb_ref[h], preferred_element_type=jnp.float32
        ).astype(jnp.bfloat16)


def queries(q_nope, w_uk):
    rows = q_nope.shape[0]
    head_count = w_uk.shape[0]
    heads = min(4, head_count)
    return pl.pallas_call(
        functools.partial(query_kernel, heads),
        grid=(head_count // heads,),
        in_specs=[
            pl.BlockSpec((rows, heads * NOPE), lambda i: (0, i)),
            pl.BlockSpec((heads, NOPE, LATENT), lambda i: (i, 0, 0)),
        ],
        out_specs=pl.BlockSpec((heads, rows, LATENT), lambda i: (i, 0, 0)),
        out_shape=jax.ShapeDtypeStruct((head_count, rows, LATENT), jnp.bfloat16),
        compiler_params=pltpu.CompilerParams(vmem_limit_bytes=6 * 1024 * 1024),
        cost_estimate=pl.CostEstimate(
            flops=2 * head_count * rows * NOPE * LATENT, bytes_accessed=6 * 1024 * 1024, transcendentals=0
        ),
        name="queries",
    )(in_hbm(q_nope), in_hbm(w_uk))


def assemble_kernel(*refs):
    tile_refs, out_ref = refs[:-1], refs[-1]
    half = tile_refs[0].shape[1]
    for t, tile_ref in enumerate(tile_refs):
        out_ref[:, t * half : (t + 1) * half] = tile_ref[...]


def assemble(tiles):
    depth, half = tiles[0].shape
    vmem = pl.BlockSpec(memory_space=pltpu.VMEM)
    return pl.pallas_call(
        assemble_kernel,
        in_specs=[vmem] * len(tiles),
        out_specs=vmem,
        out_shape=jax.ShapeDtypeStruct((depth, half * len(tiles)), jnp.bfloat16),
        compiler_params=pltpu.CompilerParams(vmem_limit_bytes=4 * 1024 * 1024),
        cost_estimate=pl.CostEstimate(
            flops=1000000, bytes_accessed=4 * depth * half * len(tiles), transcendentals=0
        ),
        name="assemble",
    )(*tiles)


def attention_kernel(
    heads, chunk, block_ref, pos_ref, latent_ref, rope_ref, up_ref, keys_ref, out_ref, limit_ref
):
    half = PANEL // 2
    tiles = keys_ref.shape[1] // half
    rows = limit_ref.shape[0]
    my_row = lax.axis_index("row")
    side = lax.axis_index("head") & 1

    @pl.when(pl.program_id(0) == 0)
    def _():
        across = lax.broadcasted_iota(jnp.int32, (rows, rows), 1)
        down = lax.broadcasted_iota(jnp.int32, (rows, rows), 0)
        pos = pos_ref[:, chunk * rows : (chunk + 1) * rows]
        limit_ref[...] = jnp.sum(jnp.where(across == down, pos, 0), axis=1, keepdims=True)

    lane = lax.broadcasted_iota(jnp.int32, (1, half), 1)
    limit = limit_ref[...]
    shown = []
    for t in range(tiles):
        start = block_ref[my_row ^ (t % (tiles // 2))] * PANEL
        start = start + (side if t < tiles // 2 else 1 - side) * half
        shown.append(start + lane <= limit)
    group = max(1, min(heads, 256 // rows))
    for first in range(0, heads, group):
        query = latent_ref[first : first + group].reshape(group * rows, LATENT)
        rope = jnp.concatenate(
            [rope_ref[:, (first + g) * ROPE : (first + g + 1) * ROPE] for g in range(group)], axis=0
        )
        scores = jnp.dot(query, keys_ref[:LATENT], preferred_element_type=jnp.float32)
        scores = scores + jnp.dot(rope, keys_ref[LATENT:], preferred_element_type=jnp.float32)
        masked = []
        for t in range(tiles):
            part = scores[:, t * half : (t + 1) * half].reshape(group, rows, half)
            masked.append(jnp.where(shown[t][None], part, -jnp.inf).reshape(group * rows, half))
        scores = jnp.concatenate(masked, axis=1)
        top = jnp.max(scores, axis=1, keepdims=True)
        weights = jnp.exp2((scores - top) * (softmax_scale * 1.4426950408889634))
        denominator = jnp.sum(weights, axis=1, keepdims=True)
        mixed = lax.dot_general(
            weights.astype(jnp.bfloat16),
            keys_ref[:LATENT],
            (((1,), (1,)), ((), ())),
            preferred_element_type=jnp.float32,
        )
        mixed = (mixed / denominator).astype(jnp.bfloat16)
        for g in range(group):
            value = jnp.dot(
                mixed[g * rows : (g + 1) * rows], up_ref[first + g], preferred_element_type=jnp.float32
            )
            out_ref[:, (first + g) * VHEAD : (first + g + 1) * VHEAD] = value.astype(jnp.bfloat16)


def attention(panel_block, query_pos, query_latent, q_rope, w_uv, keys, chunk, chunks):
    head_count, all_rows, _ = query_latent.shape
    rows = all_rows // chunks
    heads = min(4, head_count)
    depth, cache = keys.shape
    flops = 2 * head_count * rows * (cache * (depth + LATENT) + LATENT * VHEAD)
    whole = lambda i: (0, 0)
    return pl.pallas_call(
        functools.partial(attention_kernel, heads, chunk),
        grid=(head_count // heads,),
        in_specs=[
            pl.BlockSpec(memory_space=pltpu.SMEM),
            pl.BlockSpec((1, all_rows), whole),
            pl.BlockSpec((heads, rows, LATENT), lambda i: (i, chunk, 0)),
            pl.BlockSpec((rows, heads * ROPE), lambda i: (chunk, i)),
            pl.BlockSpec((heads, LATENT, VHEAD), lambda i: (i, 0, 0)),
            pl.BlockSpec(memory_space=pltpu.VMEM),
        ],
        out_specs=pl.BlockSpec((rows, heads * VHEAD), lambda i: (0, i)),
        out_shape=jax.ShapeDtypeStruct((rows, head_count * VHEAD), jnp.bfloat16),
        scratch_shapes=[pltpu.VMEM((rows, 1), jnp.int32)],
        compiler_params=pltpu.CompilerParams(vmem_limit_bytes=16 * 1024 * 1024),
        cost_estimate=pl.CostEstimate(
            flops=flops, bytes_accessed=8 * 1024 * 1024, transcendentals=head_count * rows * cache
        ),
        name="attention",
    )(panel_block, query_pos.reshape(1, all_rows), query_latent, q_rope, in_hbm(w_uv), keys)


def project_kernel(sub, parts, blocks, *refs):
    values_refs, (w_ref, sent_ref, kept_ref) = refs[:parts], refs[parts:]
    upper = (lax.axis_index("head") & 1) == 1
    features = w_ref.shape[0]
    tiles = [slice(first, min(first + 256, features)) for first in range(0, features, 256)]
    values = jnp.concatenate([r[...] for r in values_refs], axis=0) if parts > 1 else values_refs[0][...]
    for tile in tiles:
        product = lax.dot_general(
            values, w_ref[tile], (((1,), (1,)), ((), ())), preferred_element_type=jnp.float32
        )
        pairs = product.reshape(blocks, -1, 2, sub, product.shape[1])
        kept_ref[:, :, :, tile] = jnp.where(upper, pairs[:, :, 1], pairs[:, :, 0])
        sent_ref[:, :, :, tile] = jnp.where(upper, pairs[:, :, 0], pairs[:, :, 1]).astype(jnp.bfloat16)


def project(blocks, w_out, sub):
    parts = [chunk for block in blocks for chunk in block]
    rows = sum(chunk.shape[0] for chunk in blocks[0])
    features, depth = w_out.shape
    shape = (len(blocks), rows // (2 * sub), sub, features)
    vmem = pl.BlockSpec(memory_space=pltpu.VMEM)
    return pl.pallas_call(
        functools.partial(project_kernel, sub, len(parts), len(blocks)),
        in_specs=[vmem] * (len(parts) + 1),
        out_specs=[vmem, vmem],
        compiler_params=pltpu.CompilerParams(vmem_limit_bytes=(1 + len(blocks)) * 1024 * 1024),
        out_shape=[jax.ShapeDtypeStruct(shape, jnp.bfloat16), jax.ShapeDtypeStruct(shape, jnp.float32)],
        cost_estimate=pl.CostEstimate(
            flops=2 * len(blocks) * rows * depth * features,
            bytes_accessed=2 * depth * (features + rows),
            transcendentals=0,
        ),
        name="project",
    )(*parts, w_out)


def pair_kernel(kept_ref, come_ref, *out_refs):
    chip = lax.axis_index("head") >> 1
    for j, out_ref in enumerate(out_refs):
        at = chip ^ j
        total = kept_ref[:, pl.ds(at, 1)] + come_ref[:, pl.ds(at, 1)].astype(jnp.float32)
        out_ref[...] = total[:, 0].astype(out_ref.dtype)


def pair_sum(kept, come):
    blocks, count, sub, features = kept.shape
    vmem = pl.BlockSpec(memory_space=pltpu.VMEM)
    return pl.pallas_call(
        pair_kernel,
        in_specs=[vmem, vmem],
        out_specs=[vmem] * count,
        compiler_params=pltpu.CompilerParams(vmem_limit_bytes=2 * 1024 * 1024),
        out_shape=[
            jax.ShapeDtypeStruct((blocks, sub, features), jnp.bfloat16 if j else jnp.float32)
            for j in range(count)
        ],
        cost_estimate=pl.CostEstimate(
            flops=blocks * count * sub * features,
            bytes_accessed=6 * blocks * count * sub * features,
            transcendentals=0,
        ),
        name="pair_sum",
    )(kept, come)


def chip_kernel(*refs):
    count = refs[0].shape[0]
    terms, outs = refs[:-count], refs[-count:]
    for b, out_ref in enumerate(outs):
        total = terms[0][b]
        for term in terms[1:]:
            total = total + term[b].astype(jnp.float32)
        out_ref[...] = total.astype(jnp.bfloat16)


def chip_sum(terms):
    blocks, sub, features = terms[0].shape
    vmem = pl.BlockSpec(memory_space=pltpu.VMEM)
    return pl.pallas_call(
        chip_kernel,
        in_specs=[vmem] * len(terms),
        out_specs=[vmem] * blocks,
        compiler_params=pltpu.CompilerParams(vmem_limit_bytes=2 * 1024 * 1024),
        out_shape=[jax.ShapeDtypeStruct((sub, features), jnp.bfloat16)] * blocks,
        cost_estimate=pl.CostEstimate(
            flops=len(terms) * blocks * sub * features,
            bytes_accessed=2 * len(terms) * blocks * sub * features,
            transcendentals=0,
        ),
        name="chip_sum",
    )(*terms)


def finish_kernel(*refs):
    pieces, out_ref = refs[:-1], refs[-1]
    width = pieces[0].shape[1]
    my_row = lax.axis_index("row")
    for k, piece_ref in enumerate(pieces):
        columns = pl.ds(pl.multiple_of((my_row ^ k) * width, width), width)
        out_ref[:, columns] = piece_ref[...]


def finish(pieces):
    sub, width = pieces[0].shape
    if width % 128:
        out = jnp.zeros((sub, width * len(pieces)), jnp.bfloat16)
        for k, piece in enumerate(pieces):
            out = lax.dynamic_update_slice(out, piece, (0, (lax.axis_index("row") ^ k) * width))
        return out
    vmem = pl.BlockSpec(memory_space=pltpu.VMEM)
    return pl.pallas_call(
        finish_kernel,
        in_specs=[vmem] * len(pieces),
        out_specs=vmem,
        compiler_params=pltpu.CompilerParams(vmem_limit_bytes=2 * 1024 * 1024),
        out_shape=jax.ShapeDtypeStruct((sub, width * len(pieces)), jnp.bfloat16),
        name="finish",
    )(*pieces)


def on_device(q_nope, q_rope, latent_keys, rope_keys, panel_block, query_pos, w_uk, w_uv, w_out):
    row_devices = lax.axis_size("row")
    sub_rows = q_nope.shape[0] // lax.axis_size("head")

    mine = panel_half(latent_keys, rope_keys)
    halves = [block[0] for block in gather_blocks([mine])]
    others = [swap(h, "head", 1) for h in halves]
    query_latent = queries(q_nope, w_uk)
    keys = assemble(halves + others)
    chunks = 2
    values = []
    for c in range(chunks):
        values.append(attention(panel_block, query_pos, query_latent, q_rope, w_uv, keys, c, chunks))

    blocks = gather_blocks(values)
    w_out = load(w_out)
    pieces = []
    groups = [list(range(row_devices - 1)), [row_devices - 1]]
    for group in groups:
        sent, kept = project([blocks[k] for k in group], w_out, sub_rows)
        sums = pair_sum(kept, swap(sent, "head", 1))
        terms = [sums[0]]
        for j in range(1, len(sums)):
            terms.append(swap(sums[j], "head", 2 * j))
        for k, total in zip(group, chip_sum(terms)):
            pieces.append(swap(total, "row", k) if k else total)
    return finish(pieces)


def solution(mesh):
    return jax.shard_map(
        on_device,
        mesh=mesh,
        in_specs=(
            P("row", "head"),
            P("row", "head"),
            P(None, "row"),
            P(None, "row"),
            P(),
            P("row"),
            P("head", None, None),
            P("head", None, None),
            P("row", "head"),
        ),
        out_specs=P(("row", "head"), None),
        check_vma=False,
    )
```

profile of v0, /device:TPU:0, one launch (start us, length us, event | category | flops | bytes accessed | tf_op | source)
XLA Modules:
  0.0 109.4 jit_solution(14131067577031155520)
XLA Ops:
  0.0 0.9 panel_half.1.refs_0_
  0.9 4.1 %collective-permute-start.1 = (bf16[576,128]{1,0:T(8,128)(2,1)S(1)}, bf16[576,128]{1,0:T(8,128)(2,1)S(1)}, u32[]{:S(2)}, u32[]{:S(2)}) collective-permute-start(bf16[576,128]{1,0:T(8,128)(2,1)S(1)} %panel_half.1.refs_0_), channel_id=1, source_target_pairs={{0,16},{8,24},{16,0},{24,8},{1,17},{9,25},{17,1},{25,9},{2,18},{10... | collective-permute-start | bytes 442376 | tf_op jit(solution)/shard_map/ppermute | solution.py:27
  5.1 1.6 %collective-permute-start = (bf16[576,128]{1,0:T(8,128)(2,1)S(1)}, bf16[576,128]{1,0:T(8,128)(2,1)S(1)}, u32[]{:S(2)}, u32[]{:S(2)}) collective-permute-start(bf16[576,128]{1,0:T(8,128)(2,1)S(1)} %panel_half.1.refs_0_), channel_id=1, source_target_pairs={{0,8},{8,0},{16,24},{24,16},{1,9},{9,1},{17,25},{25,17},{2,10},{10... | collective-permute-start | bytes 442376 | tf_op jit(solution)/shard_map/ppermute | solution.py:27
  6.6 5.5 %collective-permute-done.1.refs_2_ = bf16[576,128]{1,0:T(8,128)(2,1)S(1)} collective-permute-done((bf16[576,128]{1,0:T(8,128)(2,1)S(1)}, bf16[576,128]{1,0:T(8,128)(2,1)S(1)}, u32[]{:S(2)}, u32[]{:S(2)}) %collective-permute-start.1) | collective-permute-done | bytes 147488 | tf_op jit(solution)/shard_map/ppermute | solution.py:27
  12.2 0.6 collective-permute-start.2
  12.8 0.0 collective-permute-start.3
  12.8 0.5 collective-permute-start.5
  13.3 0.0 collective-permute-done.refs_1_
  13.3 0.0 collective-permute-start.4
  13.3 4.0 %collective-permute-done.2.refs_3_ = bf16[576,128]{1,0:T(8,128)(2,1)S(1)} collective-permute-done((bf16[576,128]{1,0:T(8,128)(2,1)S(1)}, bf16[576,128]{1,0:T(8,128)(2,1)S(1)}, u32[]{:S(2)}, u32[]{:S(2)}) %collective-permute-start.2) | collective-permute-done | bytes 147488 | tf_op jit(solution)/shard_map/ppermute | solution.py:27
  17.3 0.0 collective-permute-start.6
  17.3 3.1 %queries.1.latent_ref = bf16[16,128,512]{2,1,0:T(8,128)(2,1)S(1)} custom-call(bf16[128,2048]{1,0:T(8,128)(2,1)} %nope_ref.1, bf16[16,128,512]{2,1,0:T(8,128)(2,1)} %absorb_ref.1), custom_call_target="tpu_custom_call" | custom-call | flops 268435456 | bytes 6291456 | tf_op jit(solution)/shard_map/queries/pallas_call | solution.py:102
  20.5 0.0 copy-start
  20.5 0.0 copy-start.1
  20.5 0.0 copy-start.2
  20.5 0.0 collective-permute-done.3.refs_4_
  20.5 0.0 collective-permute-done.4.refs_5_
  20.5 0.0 collective-permute-done.5.refs_6_
  20.5 0.0 collective-permute-done.6.refs_7_
  20.5 0.3 assemble.1.keys_ref
  20.9 0.5 copy-done
  21.4 0.0 copy-done.2
  21.4 6.3 %attention.2.refs_0_ = bf16[64,2048]{1,0:T(8,128)(2,1)S(1)} custom-call(s32[4]{0:T(128)S(1)} %copy-done.1, s32[1,128]{1,0:T(1,128)S(1)} %bitcast.1, bf16[16,128,512]{2,1,0:T(8,128)(2,1)S(1)} %queries.1.latent_ref, bf16[128,1024]{1,0:T(8,128)(2,1)S(1)} %copy-done, bf16[16,512,128]{2,1,0:T(8,128)(2,1)} %up_ref.3, bf16[576,1024]{1,0:T(8,128)(2,1)S(1)} %assemble.1.keys_ref), custom_call_target="tpu_custom_call" | custom-call | flops 2415919104 | bytes 8388608 | tf_op jit(solution)/shard_map/attention/pallas_call | solution.py:202
  27.7 6.3 %attention.3.refs_1_ = bf16[64,2048]{1,0:T(8,128)(2,1)S(1)} custom-call(s32[4]{0:T(128)S(1)} %copy-done.1, s32[1,128]{1,0:T(1,128)S(1)} %bitcast.2, bf16[16,128,512]{2,1,0:T(8,128)(2,1)S(1)} %queries.1.latent_ref, bf16[128,1024]{1,0:T(8,128)(2,1)S(1)} %copy-done, bf16[16,512,128]{2,1,0:T(8,128)(2,1)} %up_ref.3, bf16[576,1024]{1,0:T(8,128)(2,1)S(1)} %assemble.1.keys_ref), custom_call_target="tpu_custom_call" | custom-call | flops 2415919104 | bytes 8388608 | tf_op jit(solution)/shard_map/attention/pallas_call | solution.py:202
  34.0 1.3 %collective-permute-start.7 = (bf16[64,2048]{1,0:T(8,128)(2,1)S(1)}, bf16[64,2048]{1,0:T(8,128)(2,1)S(1)}, u32[]{:S(2)}, u32[]{:S(2)}) collective-permute-start(bf16[64,2048]{1,0:T(8,128)(2,1)S(1)} %attention.2.refs_0_), channel_id=1, source_target_pairs={{0,8},{8,0},{16,24},{24,16},{1,9},{9,1},{17,25},{25,17},{2,10},{10... | collective-permute-start | bytes 786440 | tf_op jit(solution)/shard_map/ppermute | solution.py:27
  35.4 0.8 collective-permute-start.8
  36.1 2.9 %collective-permute-start.9 = (bf16[64,2048]{1,0:T(8,128)(2,1)S(1)}, bf16[64,2048]{1,0:T(8,128)(2,1)S(1)}, u32[]{:S(2)}, u32[]{:S(2)}) collective-permute-start(bf16[64,2048]{1,0:T(8,128)(2,1)S(1)} %attention.2.refs_0_), channel_id=1, source_target_pairs={{0,16},{8,24},{16,0},{24,8},{1,17},{9,25},{17,1},{25,9},{2,18},{10... | collective-permute-start | bytes 786440 | tf_op jit(solution)/shard_map/ppermute | solution.py:27
  39.0 0.0 collective-permute-start.10
  39.1 3.1 %load.1.refs_6_.refs_2_ = bf16[1792,2048]{1,0:T(8,128)(2,1)S(1)} custom-call(bf16[1792,2048]{1,0:T(8,128)(2,1)} %hbm_ref.1), custom_call_target="tpu_custom_call" | custom-call | flops 4000000 | bytes 7340032 | tf_op jit(solution)/shard_map/load/pallas_call | solution.py:79
  42.2 12.1 %collective-permute-done.7.refs_2_ = bf16[64,2048]{1,0:T(8,128)(2,1)S(1)} collective-permute-done((bf16[64,2048]{1,0:T(8,128)(2,1)S(1)}, bf16[64,2048]{1,0:T(8,128)(2,1)S(1)}, u32[]{:S(2)}, u32[]{:S(2)}) %collective-permute-start.7) | collective-permute-done | bytes 262176 | tf_op jit(solution)/shard_map/ppermute | solution.py:27
  54.2 5.2 %collective-permute-done.8.refs_3_ = bf16[64,2048]{1,0:T(8,128)(2,1)S(1)} collective-permute-done((bf16[64,2048]{1,0:T(8,128)(2,1)S(1)}, bf16[64,2048]{1,0:T(8,128)(2,1)S(1)}, u32[]{:S(2)}, u32[]{:S(2)}) %collective-permute-start.8) | collective-permute-done | bytes 262176 | tf_op jit(solution)/shard_map/ppermute | solution.py:27
  59.4 0.0 collective-permute-done.9.refs_4_
  59.4 3.1 %collective-permute-done.10.refs_5_ = bf16[64,2048]{1,0:T(8,128)(2,1)S(1)} collective-permute-done((bf16[64,2048]{1,0:T(8,128)(2,1)S(1)}, bf16[64,2048]{1,0:T(8,128)(2,1)S(1)}, u32[]{:S(2)}, u32[]{:S(2)}) %collective-permute-start.10) | collective-permute-done | bytes 262176 | tf_op jit(solution)/shard_map/ppermute | solution.py:27
  62.4 3.0 %project.2 = (bf16[3,4,16,1792]{3,2,1,0:T(8,128)(2,1)S(1)}, f32[3,4,16,1792]{3,2,1,0:T(8,128)S(1)}) custom-call(bf16[64,2048]{1,0:T(8,128)(2,1)S(1)} %attention.2.refs_0_, bf16[64,2048]{1,0:T(8,128)(2,1)S(1)} %attention.3.refs_1_, bf16[64,2048]{1,0:T(8,128)(2,1)S(1)} %collective-permute-done.7.refs_2_, bf16[64,2048]{1,0:T(8,128)(2,1)S(1)} %collective-permute-done.8.refs_3_, ...), custom_call_target="tpu_custom_call" | custom-call | flops 2818572288 | bytes 7864320 | tf_op jit(solution)/shard_map/project/pallas_call | solution.py:245
  65.5 0.1 collective-permute-start.11
  65.6 1.0 collective-permute-start.17
  66.5 1.1 %collective-permute-start.18 = (bf16[64,2048]{1,0:T(8,128)(2,1)S(1)}, bf16[64,2048]{1,0:T(8,128)(2,1)S(1)}, u32[]{:S(2)}, u32[]{:S(2)}) collective-permute-start(bf16[64,2048]{1,0:T(8,128)(2,1)S(1)} %collective-permute-done.10.refs_5_), channel_id=1, source_target_pairs={{0,8},{8,0},{16,24},{24,16},{1,9},{9,1},{17,25},{25,17},{2,10},{10... | collective-permute-start | bytes 786440 | tf_op jit(solution)/shard_map/ppermute | solution.py:27
  67.6 7.2 %collective-permute-done.17.refs_0_ = bf16[64,2048]{1,0:T(8,128)(2,1)S(1)} collective-permute-done((bf16[64,2048]{1,0:T(8,128)(2,1)S(1)}, bf16[64,2048]{1,0:T(8,128)(2,1)S(1)}, u32[]{:S(2)}, u32[]{:S(2)}) %collective-permute-start.17) | collective-permute-done | bytes 262176 | tf_op jit(solution)/shard_map/ppermute | solution.py:27
  74.8 5.1 %collective-permute-done.18.refs_1_ = bf16[64,2048]{1,0:T(8,128)(2,1)S(1)} collective-permute-done((bf16[64,2048]{1,0:T(8,128)(2,1)S(1)}, bf16[64,2048]{1,0:T(8,128)(2,1)S(1)}, u32[]{:S(2)}, u32[]{:S(2)}) %collective-permute-start.18) | collective-permute-done | bytes 262176 | tf_op jit(solution)/shard_map/ppermute | solution.py:27
  79.9 2.5 %project.3 = (bf16[1,4,16,1792]{3,2,1,0:T(8,128)(2,1)S(1)}, f32[1,4,16,1792]{3,2,1,0:T(8,128)S(1)}) custom-call(bf16[64,2048]{1,0:T(8,128)(2,1)S(1)} %collective-permute-done.17.refs_0_, bf16[64,2048]{1,0:T(8,128)(2,1)S(1)} %collective-permute-done.18.refs_1_, bf16[1792,2048]{1,0:T(8,128)(2,1)S(1)} %load.1.refs_6_.refs_2_), custom_call_target="tpu_custom_call" | custom-call | flops 939524096 | bytes 7864320 | tf_op jit(solution)/shard_map/project/pallas_call | solution.py:245
  82.4 0.1 collective-permute-start.19
  82.5 0.0 collective-permute-done.11.come_ref
  82.5 0.1 pair_sum.2
  82.6 1.6 %collective-permute-start.12 = (bf16[3,16,1792]{2,1,0:T(8,128)(2,1)S(1)}, bf16[3,16,1792]{2,1,0:T(8,128)(2,1)S(1)}, u32[]{:S(2)}, u32[]{:S(2)}) collective-permute-start(bf16[3,16,1792]{2,1,0:T(8,128)(2,1)S(1)} %get-tuple-element.23), channel_id=1, source_target_pairs={{0,2},{1,3},{2,0},{3,1},{4,6},{5,7},{6,4},{7,5},{8,10},{9,11},{10,... | collective-permute-start | bytes 516104 | tf_op jit(solution)/shard_map/ppermute | solution.py:27
  84.2 1.5 %collective-permute-start.13 = (bf16[3,16,1792]{2,1,0:T(8,128)(2,1)S(1)}, bf16[3,16,1792]{2,1,0:T(8,128)(2,1)S(1)}, u32[]{:S(2)}, u32[]{:S(2)}) collective-permute-start(bf16[3,16,1792]{2,1,0:T(8,128)(2,1)S(1)} %get-tuple-element.24), channel_id=1, source_target_pairs={{0,4},{1,5},{2,6},{3,7},{4,0},{5,1},{6,2},{7,3},{8,12},{9,13},{10,... | collective-permute-start | bytes 516104 | tf_op jit(solution)/shard_map/ppermute | solution.py:27
  85.7 0.5 collective-permute-start.14
  86.2 0.0 collective-permute-done.19.come_ref
  86.2 1.6 %collective-permute-start.20 = (bf16[1,16,1792]{2,1,0:T(8,128)(2,1)S(1)}, bf16[1,16,1792]{2,1,0:T(8,128)(2,1)S(1)}, u32[]{:S(2)}, u32[]{:S(2)}) collective-permute-start(bf16[1,16,1792]{2,1,0:T(8,128)(2,1)S(1)} %get-tuple-element.32), channel_id=1, source_target_pairs={{0,2},{1,3},{2,0},{3,1},{4,6},{5,7},{6,4},{7,5},{8,10},{9,11},{10,... | collective-permute-start | bytes 172040 | tf_op jit(solution)/shard_map/ppermute | solution.py:27
  87.8 1.5 %collective-permute-start.21 = (bf16[1,16,1792]{2,1,0:T(8,128)(2,1)S(1)}, bf16[1,16,1792]{2,1,0:T(8,128)(2,1)S(1)}, u32[]{:S(2)}, u32[]{:S(2)}) collective-permute-start(bf16[1,16,1792]{2,1,0:T(8,128)(2,1)S(1)} %get-tuple-element.33), channel_id=1, source_target_pairs={{0,4},{1,5},{2,6},{3,7},{4,0},{5,1},{6,2},{7,3},{8,12},{9,13},{10,... | collective-permute-start | bytes 172040 | tf_op jit(solution)/shard_map/ppermute | solution.py:27
  89.3 5.1 %collective-permute-done.20.refs_1_ = bf16[1,16,1792]{2,1,0:T(8,128)(2,1)S(1)} collective-permute-done((bf16[1,16,1792]{2,1,0:T(8,128)(2,1)S(1)}, bf16[1,16,1792]{2,1,0:T(8,128)(2,1)S(1)}, u32[]{:S(2)}, u32[]{:S(2)}) %collective-permute-start.20) | collective-permute-done | bytes 57376 | tf_op jit(solution)/shard_map/ppermute | solution.py:27
  94.4 2.4 %collective-permute-start.22 = (bf16[1,16,1792]{2,1,0:T(8,128)(2,1)S(1)}, bf16[1,16,1792]{2,1,0:T(8,128)(2,1)S(1)}, u32[]{:S(2)}, u32[]{:S(2)}) collective-permute-start(bf16[1,16,1792]{2,1,0:T(8,128)(2,1)S(1)} %get-tuple-element.34), channel_id=1, source_target_pairs={{0,6},{1,7},{2,4},{3,5},{4,2},{5,3},{6,0},{7,1},{8,14},{9,15},{10,... | collective-permute-start | bytes 172040 | tf_op jit(solution)/shard_map/ppermute | solution.py:27
  96.8 0.0 collective-permute-done.21.refs_2_
  96.8 2.6 %collective-permute-done.22.refs_3_ = bf16[1,16,1792]{2,1,0:T(8,128)(2,1)S(1)} collective-permute-done((bf16[1,16,1792]{2,1,0:T(8,128)(2,1)S(1)}, bf16[1,16,1792]{2,1,0:T(8,128)(2,1)S(1)}, u32[]{:S(2)}, u32[]{:S(2)}) %collective-permute-start.22) | collective-permute-done | bytes 57376 | tf_op jit(solution)/shard_map/ppermute | solution.py:27
  99.5 3.8 %collective-permute-start.23 = (bf16[16,1792]{1,0:T(8,128)(2,1)S(1)}, bf16[16,1792]{1,0:T(8,128)(2,1)S(1)}, u32[]{:S(2)}, u32[]{:S(2)}) collective-permute-start(bf16[16,1792]{1,0:T(8,128)(2,1)S(1)} %chip_sum.3), channel_id=1, source_target_pairs={{0,24},{8,16},{16,8},{24,0},{1,25},{9,17},{17,9},{25,1},{2,26},{10... | collective-permute-start | bytes 172040 | tf_op jit(solution)/shard_map/ppermute | solution.py:27
  103.3 0.0 collective-permute-done.12.refs_1_
  103.3 0.0 collective-permute-done.13.refs_2_
  103.3 0.0 collective-permute-done.14.refs_3_
  103.3 0.1 chip_sum.2
  103.4 0.1 collective-permute-start.15
  103.5 0.6 collective-permute-start.16
  104.1 1.4 %collective-permute-done.23.refs_3_ = bf16[16,1792]{1,0:T(8,128)(2,1)S(1)} collective-permute-done((bf16[16,1792]{1,0:T(8,128)(2,1)S(1)}, bf16[16,1792]{1,0:T(8,128)(2,1)S(1)}, u32[]{:S(2)}, u32[]{:S(2)}) %collective-permute-start.23) | collective-permute-done | bytes 57376 | tf_op jit(solution)/shard_map/ppermute | solution.py:27
  105.6 2.1 %collective-permute-done.15.refs_1_ = bf16[16,1792]{1,0:T(8,128)(2,1)S(1)} collective-permute-done((bf16[16,1792]{1,0:T(8,128)(2,1)S(1)}, bf16[16,1792]{1,0:T(8,128)(2,1)S(1)}, u32[]{:S(2)}, u32[]{:S(2)}) %collective-permute-start.15) | collective-permute-done | bytes 57376 | tf_op jit(solution)/shard_map/ppermute | solution.py:27
  107.7 1.0 collective-permute-done.16.refs_2_
  108.7 0.7 finish.1
  (3 shorter events, 0.1 us)
Async XLA Ops:
  0.9 11.2 %collective-permute-start.1 = (bf16[576,128]{1,0:T(8,128)(2,1)S(1)}, bf16[576,128]{1,0:T(8,128)(2,1)S(1)}, u32[]{:S(2)}, u32[]{:S(2)}) collective-permute-start(bf16[576,128]{1,0:T(8,128)(2,1)S(1)} %panel_half.1.refs_0_), channel_id=1, source_target_pairs={{0,16},{8,24},{16,0},{24,8},{1,17},{9,25},{17,1},{25,9},{2,18},{10... | collective-permute-start | bytes 442376 | tf_op jit(solution)/shard_map/ppermute | solution.py:27
  5.1 8.2 %collective-permute-start = (bf16[576,128]{1,0:T(8,128)(2,1)S(1)}, bf16[576,128]{1,0:T(8,128)(2,1)S(1)}, u32[]{:S(2)}, u32[]{:S(2)}) collective-permute-start(bf16[576,128]{1,0:T(8,128)(2,1)S(1)} %panel_half.1.refs_0_), channel_id=1, source_target_pairs={{0,8},{8,0},{16,24},{24,16},{1,9},{9,1},{17,25},{25,17},{2,10},{10... | collective-permute-start | bytes 442376 | tf_op jit(solution)/shard_map/ppermute | solution.py:27
  12.2 5.1 %collective-permute-start.2 = (bf16[576,128]{1,0:T(8,128)(2,1)S(1)}, bf16[576,128]{1,0:T(8,128)(2,1)S(1)}, u32[]{:S(2)}, u32[]{:S(2)}) collective-permute-start(bf16[576,128]{1,0:T(8,128)(2,1)S(1)} %collective-permute-done.1.refs_2_), channel_id=1, source_target_pairs={{0,8},{8,0},{16,24},{24,16},{1,9},{9,1},{17,25},{25,17},{2,10},{10... | collective-permute-start | bytes 442376 | tf_op jit(solution)/shard_map/ppermute | solution.py:27
  12.8 7.7 %collective-permute-start.3 = (bf16[576,128]{1,0:T(8,128)(2,1)S(1)}, bf16[576,128]{1,0:T(8,128)(2,1)S(1)}, u32[]{:S(2)}, u32[]{:S(2)}) collective-permute-start(bf16[576,128]{1,0:T(8,128)(2,1)S(1)} %panel_half.1.refs_0_), channel_id=1, source_target_pairs={{0,1},{1,0},{2,3},{3,2},{4,5},{5,4},{6,7},{7,6},{8,9},{9,8},{10,11... | collective-permute-start | bytes 442376 | tf_op jit(solution)/shard_map/ppermute | solution.py:27
  12.8 7.7 %collective-permute-start.5 = (bf16[576,128]{1,0:T(8,128)(2,1)S(1)}, bf16[576,128]{1,0:T(8,128)(2,1)S(1)}, u32[]{:S(2)}, u32[]{:S(2)}) collective-permute-start(bf16[576,128]{1,0:T(8,128)(2,1)S(1)} %collective-permute-done.1.refs_2_), channel_id=1, source_target_pairs={{0,1},{1,0},{2,3},{3,2},{4,5},{5,4},{6,7},{7,6},{8,9},{9,8},{10,11... | collective-permute-start | bytes 442376 | tf_op jit(solution)/shard_map/ppermute | solution.py:27
  13.3 7.2 %collective-permute-start.4 = (bf16[576,128]{1,0:T(8,128)(2,1)S(1)}, bf16[576,128]{1,0:T(8,128)(2,1)S(1)}, u32[]{:S(2)}, u32[]{:S(2)}) collective-permute-start(bf16[576,128]{1,0:T(8,128)(2,1)S(1)} %collective-permute-done.refs_1_), channel_id=1, source_target_pairs={{0,1},{1,0},{2,3},{3,2},{4,5},{5,4},{6,7},{7,6},{8,9},{9,8},{10,11... | collective-permute-start | bytes 442376 | tf_op jit(solution)/shard_map/ppermute | solution.py:27
  17.3 3.2 %collective-permute-start.6 = (bf16[576,128]{1,0:T(8,128)(2,1)S(1)}, bf16[576,128]{1,0:T(8,128)(2,1)S(1)}, u32[]{:S(2)}, u32[]{:S(2)}) collective-permute-start(bf16[576,128]{1,0:T(8,128)(2,1)S(1)} %collective-permute-done.2.refs_3_), channel_id=1, source_target_pairs={{0,1},{1,0},{2,3},{3,2},{4,5},{5,4},{6,7},{7,6},{8,9},{9,8},{10,11... | collective-permute-start | bytes 442376 | tf_op jit(solution)/shard_map/ppermute | solution.py:27
  20.5 1.0 copy-start
  20.5 0.9 copy-start.1
  20.5 0.9 copy-start.2
  34.0 20.2 %collective-permute-start.7 = (bf16[64,2048]{1,0:T(8,128)(2,1)S(1)}, bf16[64,2048]{1,0:T(8,128)(2,1)S(1)}, u32[]{:S(2)}, u32[]{:S(2)}) collective-permute-start(bf16[64,2048]{1,0:T(8,128)(2,1)S(1)} %attention.2.refs_0_), channel_id=1, source_target_pairs={{0,8},{8,0},{16,24},{24,16},{1,9},{9,1},{17,25},{25,17},{2,10},{10... | collective-permute-start | bytes 786440 | tf_op jit(solution)/shard_map/ppermute | solution.py:27
  35.4 24.0 %collective-permute-start.8 = (bf16[64,2048]{1,0:T(8,128)(2,1)S(1)}, bf16[64,2048]{1,0:T(8,128)(2,1)S(1)}, u32[]{:S(2)}, u32[]{:S(2)}) collective-permute-start(bf16[64,2048]{1,0:T(8,128)(2,1)S(1)} %attention.3.refs_1_), channel_id=1, source_target_pairs={{0,8},{8,0},{16,24},{24,16},{1,9},{9,1},{17,25},{25,17},{2,10},{10... | collective-permute-start | bytes 786440 | tf_op jit(solution)/shard_map/ppermute | solution.py:27
  36.1 23.2 %collective-permute-start.9 = (bf16[64,2048]{1,0:T(8,128)(2,1)S(1)}, bf16[64,2048]{1,0:T(8,128)(2,1)S(1)}, u32[]{:S(2)}, u32[]{:S(2)}) collective-permute-start(bf16[64,2048]{1,0:T(8,128)(2,1)S(1)} %attention.2.refs_0_), channel_id=1, source_target_pairs={{0,16},{8,24},{16,0},{24,8},{1,17},{9,25},{17,1},{25,9},{2,18},{10... | collective-permute-start | bytes 786440 | tf_op jit(solution)/shard_map/ppermute | solution.py:27
  39.0 23.4 %collective-permute-start.10 = (bf16[64,2048]{1,0:T(8,128)(2,1)S(1)}, bf16[64,2048]{1,0:T(8,128)(2,1)S(1)}, u32[]{:S(2)}, u32[]{:S(2)}) collective-permute-start(bf16[64,2048]{1,0:T(8,128)(2,1)S(1)} %attention.3.refs_1_), channel_id=1, source_target_pairs={{0,16},{8,24},{16,0},{24,8},{1,17},{9,25},{17,1},{25,9},{2,18},{10... | collective-permute-start | bytes 786440 | tf_op jit(solution)/shard_map/ppermute | solution.py:27
  65.5 17.0 %collective-permute-start.11 = (bf16[3,4,16,1792]{3,2,1,0:T(8,128)(2,1)S(1)}, bf16[3,4,16,1792]{3,2,1,0:T(8,128)(2,1)S(1)}, u32[]{:S(2)}, u32[]{:S(2)}) collective-permute-start(bf16[3,4,16,1792]{3,2,1,0:T(8,128)(2,1)S(1)} %get-tuple-element.21), channel_id=1, source_target_pairs={{0,1},{1,0},{2,3},{3,2},{4,5},{5,4},{6,7},{7,6},{8,9},{9,8},{10,11... | collective-permute-start | bytes 2064392 | tf_op jit(solution)/shard_map/ppermute | solution.py:27
  65.6 9.2 %collective-permute-start.17 = (bf16[64,2048]{1,0:T(8,128)(2,1)S(1)}, bf16[64,2048]{1,0:T(8,128)(2,1)S(1)}, u32[]{:S(2)}, u32[]{:S(2)}) collective-permute-start(bf16[64,2048]{1,0:T(8,128)(2,1)S(1)} %collective-permute-done.9.refs_4_), channel_id=1, source_target_pairs={{0,8},{8,0},{16,24},{24,16},{1,9},{9,1},{17,25},{25,17},{2,10},{10... | collective-permute-start | bytes 786440 | tf_op jit(solution)/shard_map/ppermute | solution.py:27
  66.5 13.3 %collective-permute-start.18 = (bf16[64,2048]{1,0:T(8,128)(2,1)S(1)}, bf16[64,2048]{1,0:T(8,128)(2,1)S(1)}, u32[]{:S(2)}, u32[]{:S(2)}) collective-permute-start(bf16[64,2048]{1,0:T(8,128)(2,1)S(1)} %collective-permute-done.10.refs_5_), channel_id=1, source_target_pairs={{0,8},{8,0},{16,24},{24,16},{1,9},{9,1},{17,25},{25,17},{2,10},{10... | collective-permute-start | bytes 786440 | tf_op jit(solution)/shard_map/ppermute | solution.py:27
  82.4 3.8 %collective-permute-start.19 = (bf16[1,4,16,1792]{3,2,1,0:T(8,128)(2,1)S(1)}, bf16[1,4,16,1792]{3,2,1,0:T(8,128)(2,1)S(1)}, u32[]{:S(2)}, u32[]{:S(2)}) collective-permute-start(bf16[1,4,16,1792]{3,2,1,0:T(8,128)(2,1)S(1)} %get-tuple-element.30), channel_id=1, source_target_pairs={{0,1},{1,0},{2,3},{3,2},{4,5},{5,4},{6,7},{7,6},{8,9},{9,8},{10,11... | collective-permute-start | bytes 688136 | tf_op jit(solution)/shard_map/ppermute | solution.py:27
  82.6 20.7 %collective-permute-start.12 = (bf16[3,16,1792]{2,1,0:T(8,128)(2,1)S(1)}, bf16[3,16,1792]{2,1,0:T(8,128)(2,1)S(1)}, u32[]{:S(2)}, u32[]{:S(2)}) collective-permute-start(bf16[3,16,1792]{2,1,0:T(8,128)(2,1)S(1)} %get-tuple-element.23), channel_id=1, source_target_pairs={{0,2},{1,3},{2,0},{3,1},{4,6},{5,7},{6,4},{7,5},{8,10},{9,11},{10,... | collective-permute-start | bytes 516104 | tf_op jit(solution)/shard_map/ppermute | solution.py:27
  84.2 19.2 %collective-permute-start.13 = (bf16[3,16,1792]{2,1,0:T(8,128)(2,1)S(1)}, bf16[3,16,1792]{2,1,0:T(8,128)(2,1)S(1)}, u32[]{:S(2)}, u32[]{:S(2)}) collective-permute-start(bf16[3,16,1792]{2,1,0:T(8,128)(2,1)S(1)} %get-tuple-element.24), channel_id=1, source_target_pairs={{0,4},{1,5},{2,6},{3,7},{4,0},{5,1},{6,2},{7,3},{8,12},{9,13},{10,... | collective-permute-start | bytes 516104 | tf_op jit(solution)/shard_map/ppermute | solution.py:27
  85.7 17.7 %collective-permute-start.14 = (bf16[3,16,1792]{2,1,0:T(8,128)(2,1)S(1)}, bf16[3,16,1792]{2,1,0:T(8,128)(2,1)S(1)}, u32[]{:S(2)}, u32[]{:S(2)}) collective-permute-start(bf16[3,16,1792]{2,1,0:T(8,128)(2,1)S(1)} %get-tuple-element.25), channel_id=1, source_target_pairs={{0,6},{1,7},{2,4},{3,5},{4,2},{5,3},{6,0},{7,1},{8,14},{9,15},{10,... | collective-permute-start | bytes 516104 | tf_op jit(solution)/shard_map/ppermute | solution.py:27
  86.2 8.2 %collective-permute-start.20 = (bf16[1,16,1792]{2,1,0:T(8,128)(2,1)S(1)}, bf16[1,16,1792]{2,1,0:T(8,128)(2,1)S(1)}, u32[]{:S(2)}, u32[]{:S(2)}) collective-permute-start(bf16[1,16,1792]{2,1,0:T(8,128)(2,1)S(1)} %get-tuple-element.32), channel_id=1, source_target_pairs={{0,2},{1,3},{2,0},{3,1},{4,6},{5,7},{6,4},{7,5},{8,10},{9,11},{10,... | collective-permute-start | bytes 172040 | tf_op jit(solution)/shard_map/ppermute | solution.py:27
  87.8 9.0 %collective-permute-start.21 = (bf16[1,16,1792]{2,1,0:T(8,128)(2,1)S(1)}, bf16[1,16,1792]{2,1,0:T(8,128)(2,1)S(1)}, u32[]{:S(2)}, u32[]{:S(2)}) collective-permute-start(bf16[1,16,1792]{2,1,0:T(8,128)(2,1)S(1)} %get-tuple-element.33), channel_id=1, source_target_pairs={{0,4},{1,5},{2,6},{3,7},{4,0},{5,1},{6,2},{7,3},{8,12},{9,13},{10,... | collective-permute-start | bytes 172040 | tf_op jit(solution)/shard_map/ppermute | solution.py:27
  94.4 5.1 %collective-permute-start.22 = (bf16[1,16,1792]{2,1,0:T(8,128)(2,1)S(1)}, bf16[1,16,1792]{2,1,0:T(8,128)(2,1)S(1)}, u32[]{:S(2)}, u32[]{:S(2)}) collective-permute-start(bf16[1,16,1792]{2,1,0:T(8,128)(2,1)S(1)} %get-tuple-element.34), channel_id=1, source_target_pairs={{0,6},{1,7},{2,4},{3,5},{4,2},{5,3},{6,0},{7,1},{8,14},{9,15},{10,... | collective-permute-start | bytes 172040 | tf_op jit(solution)/shard_map/ppermute | solution.py:27
  99.5 6.1 %collective-permute-start.23 = (bf16[16,1792]{1,0:T(8,128)(2,1)S(1)}, bf16[16,1792]{1,0:T(8,128)(2,1)S(1)}, u32[]{:S(2)}, u32[]{:S(2)}) collective-permute-start(bf16[16,1792]{1,0:T(8,128)(2,1)S(1)} %chip_sum.3), channel_id=1, source_target_pairs={{0,24},{8,16},{16,8},{24,0},{1,25},{9,17},{17,9},{25,1},{2,26},{10... | collective-permute-start | bytes 172040 | tf_op jit(solution)/shard_map/ppermute | solution.py:27
  103.4 4.2 %collective-permute-start.15 = (bf16[16,1792]{1,0:T(8,128)(2,1)S(1)}, bf16[16,1792]{1,0:T(8,128)(2,1)S(1)}, u32[]{:S(2)}, u32[]{:S(2)}) collective-permute-start(bf16[16,1792]{1,0:T(8,128)(2,1)S(1)} %get-tuple-element.27), channel_id=1, source_target_pairs={{0,8},{8,0},{16,24},{24,16},{1,9},{9,1},{17,25},{25,17},{2,10},{10... | collective-permute-start | bytes 172040 | tf_op jit(solution)/shard_map/ppermute | solution.py:27
  103.5 5.1 %collective-permute-start.16 = (bf16[16,1792]{1,0:T(8,128)(2,1)S(1)}, bf16[16,1792]{1,0:T(8,128)(2,1)S(1)}, u32[]{:S(2)}, u32[]{:S(2)}) collective-permute-start(bf16[16,1792]{1,0:T(8,128)(2,1)S(1)} %get-tuple-element.28), channel_id=1, source_target_pairs={{0,16},{8,24},{16,0},{24,8},{1,17},{9,25},{17,1},{25,9},{2,18},{10... | collective-permute-start | bytes 172040 | tf_op jit(solution)/shard_map/ppermute | solution.py:27
where the time goes:
time: 110 us; the launch traced here: 109 us
  waiting for transfers between devices  54.3 us (49%)
  starting transfers between devices  27.7 us (25%)
  Pallas kernels  26.6 us (24%)
    ppermute x24, waiting for transfers between devices, swap(): return lax.ppermute(x, axis, [(i, i ^ mask) for i in range(count)])  54.3 us
    ppermute x24, starting transfers between devices, swap(): return lax.ppermute(x, axis, [(i, i ^ mask) for i in range(count)])  27.7 us
    pallas_call x2, Pallas kernels, attention(): pl.pallas_call(functools.partial(attention_kernel, heads, chunk), grid=(h...  12.6 us
    pallas_call x2, Pallas kernels, project(): pl.pallas_call(functools.partial(project_kernel, sub, len(parts), len(blo...  5.52 us
    pallas_call x1, Pallas kernels, queries(): pl.pallas_call(functools.partial(query_kernel, heads), grid=(head_count /...  3.14 us
    pallas_call x1, Pallas kernels, load(): pl.pallas_call(load_kernel, in_specs=[pl.BlockSpec(memory_space=pltpu.HBM...  3.09 us
  transfers between devices with their start and end apart: 24, of which 12 were waited for; matrix products, arithmetic and copies ran while one was open for 0% of the time, Pallas kernels for 8%

commit v1 on v0

--- a/solution.py
+++ b/solution.py
@@ -27,16 +27,18 @@
     return lax.ppermute(x, axis, [(i, i ^ mask) for i in range(count)])
 
 
-def gather_blocks(own):
+def gather_blocks(own, made=None):
+    made = made or {}
     count = lax.axis_size("row")
     blocks = {0: own}
     mask = count // 2
     while mask:
         for k in list(blocks):
+            known = list(made.get(mask, ())) if k == 0 else []
             moved = []
-            for chunk in blocks[k]:
+            for chunk in blocks[k][: len(blocks[k]) - len(known)]:
                 moved.append(swap(chunk, "row", mask))
-            blocks[k ^ mask] = moved
+            blocks[k ^ mask] = moved + known
         mask //= 2
     return [blocks[k] for k in range(count)]
 
@@ -88,8 +90,8 @@
     )(in_hbm(x))
 
 
-def query_kernel(heads, nope_ref, absorb_ref, out_ref):
-    for h in range(heads):
+def query_kernel(nope_ref, absorb_ref, out_ref):
+    for h in range(absorb_ref.shape[0]):
         out_ref[h] = jnp.dot(
             nope_ref[:, h * NOPE : (h + 1) * NOPE], absorb_ref[h], preferred_element_type=jnp.float32
         ).astype(jnp.bfloat16)
@@ -98,22 +100,67 @@
 def queries(q_nope, w_uk):
     rows = q_nope.shape[0]
     head_count = w_uk.shape[0]
-    heads = min(4, head_count)
-    return pl.pallas_call(
-        functools.partial(query_kernel, heads),
-        grid=(head_count // heads,),
-        in_specs=[
-            pl.BlockSpec((rows, heads * NOPE), lambda i: (0, i)),
-            pl.BlockSpec((heads, NOPE, LATENT), lambda i: (i, 0, 0)),
-        ],
-        out_specs=pl.BlockSpec((heads, rows, LATENT), lambda i: (i, 0, 0)),
+    vmem = pl.BlockSpec(memory_space=pltpu.VMEM)
+    return pl.pallas_call(
+        query_kernel,
+        in_specs=[vmem, vmem],
+        out_specs=vmem,
         out_shape=jax.ShapeDtypeStruct((head_count, rows, LATENT), jnp.bfloat16),
-        compiler_params=pltpu.CompilerParams(vmem_limit_bytes=6 * 1024 * 1024),
+        compiler_params=pltpu.CompilerParams(vmem_limit_bytes=4 * 1024 * 1024),
         cost_estimate=pl.CostEstimate(
             flops=2 * head_count * rows * NOPE * LATENT, bytes_accessed=6 * 1024 * 1024, transcendentals=0
         ),
         name="queries",
-    )(in_hbm(q_nope), in_hbm(w_uk))
+    )(q_nope, w_uk)
+
+
+def column_of(row):
+    size = row.shape[1]
+    across = lax.broadcasted_iota(jnp.int32, (size, size), 1)
+    down = lax.broadcasted_iota(jnp.int32, (size, size), 0)
+    return jnp.sum(jnp.where(across == down, row, 0), axis=1, keepdims=True)
+
+
+def pack_kernel(pos_ref, nope_ref, rope_ref, *rest):
+    out_refs, sems = rest[:-1], rest[-1]
+    rows, wide = nope_ref.shape
+    narrow = rope_ref.shape[1]
+    copies = []
+    for n, out_ref in enumerate(out_refs):
+        part = pl.ds(rows - out_ref.shape[0], out_ref.shape[0])
+        copies.append(pltpu.make_async_copy(nope_ref.at[part], out_ref.at[:, :wide], sems.at[2 * n]))
+        copies.append(
+            pltpu.make_async_copy(
+                rope_ref.at[part], out_ref.at[:, wide : wide + narrow], sems.at[2 * n + 1]
+            )
+        )
+    for copy in copies:
+        copy.start()
+    pos = column_of(pos_ref[...])
+    lane = lax.broadcasted_iota(jnp.int32, (rows, 128), 1)
+    coded = jnp.where(lane == 0, pos >> 8, jnp.where(lane == 1, pos & 255, 0))
+    coded = coded.astype(jnp.float32).astype(jnp.bfloat16)
+    for out_ref in out_refs:
+        out_ref[:, wide + narrow :] = coded[rows - out_ref.shape[0] :]
+    for copy in copies:
+        copy.wait()
+
+
+def pack(query_pos, q_nope, q_rope, sizes):
+    rows, wide = q_nope.shape
+    width = wide + q_rope.shape[1] + 128
+    vmem = pl.BlockSpec(memory_space=pltpu.VMEM)
+    hbm = pl.BlockSpec(memory_space=pltpu.HBM)
+    return pl.pallas_call(
+        pack_kernel,
+        in_specs=[vmem, hbm, hbm],
+        out_specs=[vmem] * len(sizes),
+        out_shape=[jax.ShapeDtypeStruct((size, width), jnp.bfloat16) for size in sizes],
+        scratch_shapes=[pltpu.SemaphoreType.DMA((2 * len(sizes),))],
+        compiler_params=pltpu.CompilerParams(vmem_limit_bytes=2 * 1024 * 1024),
+        cost_estimate=pl.CostEstimate(flops=1000000, bytes_accessed=2 * sum(sizes) * width, transcendentals=0),
+        name="pack",
+    )(query_pos.reshape(1, rows), in_hbm(q_nope), in_hbm(q_rope))
 
 
 def assemble_kernel(*refs):
@@ -139,86 +186,223 @@
     )(*tiles)
 
 
-def attention_kernel(
-    heads, chunk, block_ref, pos_ref, latent_ref, rope_ref, up_ref, keys_ref, out_ref, limit_ref
-):
+exponent_scale = softmax_scale * 1.4426950408889634
+lowest_start = -1e30
+
+
+def visible(block_ref, limit, tiles):
     half = PANEL // 2
-    tiles = keys_ref.shape[1] // half
-    rows = limit_ref.shape[0]
     my_row = lax.axis_index("row")
     side = lax.axis_index("head") & 1
-
-    @pl.when(pl.program_id(0) == 0)
-    def _():
-        across = lax.broadcasted_iota(jnp.int32, (rows, rows), 1)
-        down = lax.broadcasted_iota(jnp.int32, (rows, rows), 0)
-        pos = pos_ref[:, chunk * rows : (chunk + 1) * rows]
-        limit_ref[...] = jnp.sum(jnp.where(across == down, pos, 0), axis=1, keepdims=True)
-
     lane = lax.broadcasted_iota(jnp.int32, (1, half), 1)
-    limit = limit_ref[...]
     shown = []
-    for t in range(tiles):
-        start = block_ref[my_row ^ (t % (tiles // 2))] * PANEL
-        start = start + (side if t < tiles // 2 else 1 - side) * half
+    for k, other in tiles:
+        start = block_ref[my_row ^ k] * PANEL + ((1 - side) if other else side) * half
         shown.append(start + lane <= limit)
-    group = max(1, min(heads, 256 // rows))
-    for first in range(0, heads, group):
-        query = latent_ref[first : first + group].reshape(group * rows, LATENT)
-        rope = jnp.concatenate(
-            [rope_ref[:, (first + g) * ROPE : (first + g + 1) * ROPE] for g in range(group)], axis=0
+    return shown
+
+
+def masked_scores(latent, rope, keys, shown, rows):
+    half = PANEL // 2
+    scores = jnp.dot(jnp.concatenate((latent, rope), axis=1), keys, preferred_element_type=jnp.float32)
+    group = scores.shape[0] // rows
+    masked = []
+    for t, mask in enumerate(shown):
+        part = scores[:, t * half : (t + 1) * half].reshape(group, rows, half)
+        masked.append(jnp.where(mask[None], part, -jnp.inf).reshape(group * rows, half))
+    return jnp.concatenate(masked, axis=1)
+
+
+def mix(weights, keys):
+    return lax.dot_general(
+        weights.astype(jnp.bfloat16), keys[:LATENT], (((1,), (1,)), ((), ())), preferred_element_type=jnp.float32
+    )
+
+
+def store_values(mixed, members, rows, up_ref, out_refs):
+    for g, h in enumerate(members):
+        value = jnp.dot(mixed[g * rows : (g + 1) * rows], up_ref[h], preferred_element_type=jnp.float32)
+        value = value.astype(jnp.bfloat16)
+        done = 0
+        for out_ref in out_refs:
+            size = out_ref.shape[0]
+            out_ref[:, h * VHEAD : (h + 1) * VHEAD] = value[done : done + size]
+            done += size
+
+
+def head_groups(heads, rows):
+    group = max(1, min(heads, 512 // rows))
+    return [range(first, first + group) for first in range(0, heads, group)]
+
+
+def stacked(part_of, members):
+    return jnp.concatenate([part_of(h) for h in members], axis=0)
+
+
+def all_tiles(columns):
+    count = columns // PANEL
+    return [(k, False) for k in range(count)] + [(k, True) for k in range(count)]
+
+
+def attend(block_ref, limit, rows, latent_of, rope_of, up_ref, keys_ref, out_refs):
+    shown = visible(block_ref, limit, all_tiles(keys_ref.shape[1]))
+    for members in head_groups(up_ref.shape[0], rows):
+        scores = masked_scores(
+            stacked(latent_of, members), stacked(rope_of, members), keys_ref[...], shown, rows
         )
-        scores = jnp.dot(query, keys_ref[:LATENT], preferred_element_type=jnp.float32)
-        scores = scores + jnp.dot(rope, keys_ref[LATENT:], preferred_element_type=jnp.float32)
-        masked = []
-        for t in range(tiles):
-            part = scores[:, t * half : (t + 1) * half].reshape(group, rows, half)
-            masked.append(jnp.where(shown[t][None], part, -jnp.inf).reshape(group * rows, half))
-        scores = jnp.concatenate(masked, axis=1)
         top = jnp.max(scores, axis=1, keepdims=True)
-        weights = jnp.exp2((scores - top) * (softmax_scale * 1.4426950408889634))
+        weights = jnp.exp2((scores - top) * exponent_scale)
         denominator = jnp.sum(weights, axis=1, keepdims=True)
-        mixed = lax.dot_general(
-            weights.astype(jnp.bfloat16),
-            keys_ref[:LATENT],
-            (((1,), (1,)), ((), ())),
-            preferred_element_type=jnp.float32,
+        mixed = (mix(weights, keys_ref[...]) * (1.0 / denominator)).astype(jnp.bfloat16)
+        store_values(mixed, members, rows, up_ref, out_refs)
+
+
+def early_kernel(tiles, rows, block_ref, pos_ref, latent_ref, rope_ref, keys_ref, top_ref, sum_ref, mix_ref):
+    shown = visible(block_ref, column_of(pos_ref[...])[:rows], tiles)
+    for members in head_groups(latent_ref.shape[0], rows):
+        scores = masked_scores(
+            stacked(lambda h: latent_ref[h, :rows], members),
+            stacked(lambda h: rope_ref[:rows, h * ROPE : (h + 1) * ROPE], members),
+            keys_ref[...],
+            shown,
+            rows,
         )
-        mixed = (mixed / denominator).astype(jnp.bfloat16)
-        for g in range(group):
-            value = jnp.dot(
-                mixed[g * rows : (g + 1) * rows], up_ref[first + g], preferred_element_type=jnp.float32
-            )
-            out_ref[:, (first + g) * VHEAD : (first + g + 1) * VHEAD] = value.astype(jnp.bfloat16)
-
-
-def attention(panel_block, query_pos, query_latent, q_rope, w_uv, keys, chunk, chunks):
-    head_count, all_rows, _ = query_latent.shape
-    rows = all_rows // chunks
-    heads = min(4, head_count)
-    depth, cache = keys.shape
+        top = jnp.maximum(jnp.max(scores, axis=1, keepdims=True), lowest_start)
+        weights = jnp.exp2((scores - top) * exponent_scale)
+        at = slice(members[0] * rows, (members[-1] + 1) * rows)
+        top_ref[at] = top
+        sum_ref[at] = jnp.sum(weights, axis=1, keepdims=True)
+        mix_ref[at] = mix(weights, keys_ref[...])
+
+
+def late_kernel(
+    tiles, rows, block_ref, pos_ref, latent_ref, rope_ref, top_ref, sum_ref, mix_ref, *rest
+):
+    tile_refs, (up_ref, out_ref) = rest[: len(tiles)], rest[len(tiles) :]
+    keys = jnp.concatenate([r[...] for r in tile_refs], axis=1)
+    shown = visible(block_ref, column_of(pos_ref[...])[:rows], tiles)
+    for members in head_groups(latent_ref.shape[0], rows):
+        scores = masked_scores(
+            stacked(lambda h: latent_ref[h, :rows], members),
+            stacked(lambda h: rope_ref[:rows, h * ROPE : (h + 1) * ROPE], members),
+            keys,
+            shown,
+            rows,
+        )
+        at = slice(members[0] * rows, (members[-1] + 1) * rows)
+        top = jnp.maximum(jnp.max(scores, axis=1, keepdims=True), top_ref[at])
+        weights = jnp.exp2((scores - top) * exponent_scale)
+        before = jnp.exp2((top_ref[at] - top) * exponent_scale)
+        denominator = jnp.sum(weights, axis=1, keepdims=True) + sum_ref[at] * before
+        share = 1.0 / denominator
+        mixed = mix(weights, keys) * share + mix_ref[at] * (before * share)
+        store_values(mixed.astype(jnp.bfloat16), members, rows, up_ref, [out_ref])
+
+
+def early_attention(tiles, rows, panel_block, pos, query_latent, q_rope, keys):
+    head_count = query_latent.shape[0]
+    depth, columns = keys.shape
+    count = head_count * rows
+    vmem = pl.BlockSpec(memory_space=pltpu.VMEM)
+    return pl.pallas_call(
+        functools.partial(early_kernel, tiles, rows),
+        in_specs=[pl.BlockSpec(memory_space=pltpu.SMEM)] + [vmem] * 4,
+        out_specs=[vmem] * 3,
+        out_shape=[jax.ShapeDtypeStruct((count, size), jnp.float32) for size in (1, 1, LATENT)],
+        compiler_params=pltpu.CompilerParams(vmem_limit_bytes=12 * 1024 * 1024),
+        cost_estimate=pl.CostEstimate(
+            flops=2 * count * columns * (depth + LATENT),
+            bytes_accessed=4 * 1024 * 1024,
+            transcendentals=count * columns,
+        ),
+        name="early_attention",
+    )(panel_block, pos, query_latent, q_rope, keys)
+
+
+def late_attention(tiles, rows, panel_block, pos, query_latent, q_rope, early, arrays, w_uv):
+    head_count = query_latent.shape[0]
+    depth, columns = arrays[0].shape
+    count = head_count * rows
+    vmem = pl.BlockSpec(memory_space=pltpu.VMEM)
+    return pl.pallas_call(
+        functools.partial(late_kernel, tiles, rows),
+        in_specs=[pl.BlockSpec(memory_space=pltpu.SMEM)] + [vmem] * (7 + len(arrays)),
+        out_specs=vmem,
+        out_shape=jax.ShapeDtypeStruct((rows, head_count * VHEAD), jnp.bfloat16),
+        compiler_params=pltpu.CompilerParams(vmem_limit_bytes=12 * 1024 * 1024),
+        cost_estimate=pl.CostEstimate(
+            flops=2 * count * (columns * len(arrays) * (depth + LATENT) + LATENT * VHEAD),
+            bytes_accessed=4 * 1024 * 1024,
+            transcendentals=count * columns * len(arrays),
+        ),
+        name="late_attention",
+    )(panel_block, pos, query_latent, q_rope, *early, *arrays, w_uv)
+
+
+def own_kernel(first, rows, block_ref, pos_ref, latent_ref, rope_ref, up_ref, keys_ref, *rest):
+    part = slice(first, first + rows)
+    copy = None
+    out_refs = rest
+    if first:
+        w_ref, out_refs, held_ref, sem = rest[0], rest[1:-2], rest[-2], rest[-1]
+        copy = pltpu.make_async_copy(w_ref, held_ref, sem)
+        copy.start()
+    attend(
+        block_ref,
+        column_of(pos_ref[...])[part],
+        rows,
+        lambda h: latent_ref[h, part],
+        lambda h: rope_ref[part, h * ROPE : (h + 1) * ROPE],
+        up_ref,
+        keys_ref,
+        out_refs,
+    )
+    if copy is not None:
+        copy.wait()
+
+
+def packed_kernel(block_ref, packed_ref, absorb_ref, up_ref, keys_ref, *out_refs):
+    rows = packed_ref.shape[0]
+    heads = up_ref.shape[0]
+    wide = heads * NOPE
+    coded = packed_ref[:, wide + heads * ROPE :].astype(jnp.float32)
+    limit = (coded[:, 0:1] * 256.0 + coded[:, 1:2]).astype(jnp.int32)
+    attend(
+        block_ref,
+        limit,
+        rows,
+        lambda h: jnp.dot(
+            packed_ref[:, h * NOPE : (h + 1) * NOPE], absorb_ref[h], preferred_element_type=jnp.float32
+        ).astype(jnp.bfloat16),
+        lambda h: packed_ref[:, wide + h * ROPE : wide + (h + 1) * ROPE],
+        up_ref,
+        keys_ref,
+        out_refs,
+    )
+
+
+def attention(kernel, sizes, panel_block, *arrays, held=None):
+    head_count = arrays[-2].shape[0]
+    depth, cache = arrays[-1].shape
+    rows = sum(sizes)
     flops = 2 * head_count * rows * (cache * (depth + LATENT) + LATENT * VHEAD)
-    whole = lambda i: (0, 0)
-    return pl.pallas_call(
-        functools.partial(attention_kernel, heads, chunk),
-        grid=(head_count // heads,),
-        in_specs=[
-            pl.BlockSpec(memory_space=pltpu.SMEM),
-            pl.BlockSpec((1, all_rows), whole),
-            pl.BlockSpec((heads, rows, LATENT), lambda i: (i, chunk, 0)),
-            pl.BlockSpec((rows, heads * ROPE), lambda i: (chunk, i)),
-            pl.BlockSpec((heads, LATENT, VHEAD), lambda i: (i, 0, 0)),
-            pl.BlockSpec(memory_space=pltpu.VMEM),
-        ],
-        out_specs=pl.BlockSpec((rows, heads * VHEAD), lambda i: (0, i)),
-        out_shape=jax.ShapeDtypeStruct((rows, head_count * VHEAD), jnp.bfloat16),
-        scratch_shapes=[pltpu.VMEM((rows, 1), jnp.int32)],
+    vmem = pl.BlockSpec(memory_space=pltpu.VMEM)
+    more = [] if held is None else [held]
+    return pl.pallas_call(
+        kernel,
+        in_specs=[pl.BlockSpec(memory_space=pltpu.SMEM)]
+        + [vmem] * len(arrays)
+        + [pl.BlockSpec(memory_space=pltpu.HBM)] * len(more),
+        out_specs=[vmem] * (len(sizes) + len(more)),
+        out_shape=[jax.ShapeDtypeStruct((size, head_count * VHEAD), jnp.bfloat16) for size in sizes]
+        + [pltpu.VMEM(x.shape, x.dtype) for x in more],
+        scratch_shapes=[pltpu.SemaphoreType.DMA] * len(more),
         compiler_params=pltpu.CompilerParams(vmem_limit_bytes=16 * 1024 * 1024),
         cost_estimate=pl.CostEstimate(
             flops=flops, bytes_accessed=8 * 1024 * 1024, transcendentals=head_count * rows * cache
         ),
         name="attention",
-    )(panel_block, query_pos.reshape(1, all_rows), query_latent, q_rope, in_hbm(w_uv), keys)
+    )(panel_block, *arrays, *(in_hbm(x) for x in more))
 
 
 def project_kernel(sub, parts, blocks, *refs):
@@ -257,20 +441,26 @@
     )(*parts, w_out)
 
 
-def pair_kernel(kept_ref, come_ref, *out_refs):
+def pair_kernel(parts, *refs):
+    kept_refs, come_refs, out_refs = refs[:parts], refs[parts : 2 * parts], refs[2 * parts :]
     chip = lax.axis_index("head") >> 1
     for j, out_ref in enumerate(out_refs):
-        at = chip ^ j
-        total = kept_ref[:, pl.ds(at, 1)] + come_ref[:, pl.ds(at, 1)].astype(jnp.float32)
-        out_ref[...] = total[:, 0].astype(out_ref.dtype)
+        done = 0
+        for kept_ref, come_ref in zip(kept_refs, come_refs):
+            at = pl.ds(chip ^ j, 1)
+            total = kept_ref[:, at] + come_ref[:, at].astype(jnp.float32)
+            blocks = total.shape[0]
+            out_ref[done : done + blocks] = total[:, 0].astype(out_ref.dtype)
+            done += blocks
 
 
 def pair_sum(kept, come):
-    blocks, count, sub, features = kept.shape
-    vmem = pl.BlockSpec(memory_space=pltpu.VMEM)
-    return pl.pallas_call(
-        pair_kernel,
-        in_specs=[vmem, vmem],
+    _, count, sub, features = kept[0].shape
+    blocks = sum(k.shape[0] for k in kept)
+    vmem = pl.BlockSpec(memory_space=pltpu.VMEM)
+    return pl.pallas_call(
+        functools.partial(pair_kernel, len(kept)),
+        in_specs=[vmem] * (2 * len(kept)),
         out_specs=[vmem] * count,
         compiler_params=pltpu.CompilerParams(vmem_limit_bytes=2 * 1024 * 1024),
         out_shape=[
@@ -283,7 +473,7 @@
             transcendentals=0,
         ),
         name="pair_sum",
-    )(kept, come)
+    )(*kept, *come)
 
 
 def chip_kernel(*refs):
@@ -347,25 +537,58 @@
 
     mine = panel_half(latent_keys, rope_keys)
     halves = [block[0] for block in gather_blocks([mine])]
-    others = [swap(h, "head", 1) for h in halves]
+    others = []
+    for h in halves:
+        others.append(swap(h, "head", 1))
+    rows = q_nope.shape[0]
+    w_uk = load(w_uk)
     query_latent = queries(q_nope, w_uk)
-    keys = assemble(halves + others)
-    chunks = 2
-    values = []
-    for c in range(chunks):
-        values.append(attention(panel_block, query_pos, query_latent, q_rope, w_uv, keys, c, chunks))
-
-    blocks = gather_blocks(values)
-    w_out = load(w_out)
+    (packed,) = pack(query_pos, q_nope, q_rope, [rows // 2])
+    w_uv = load(w_uv)
+    packed = swap(packed, "row", 1)
+    pos = query_pos.reshape(1, rows)
+    last = row_devices - 1
+    tiles = all_tiles(row_devices * PANEL)
+    first_tiles = [t for t in tiles if t[0] != last]
+    last_tiles = [t for t in tiles if t[0] == last]
+    arrays_of = lambda some: [others[k] if other else halves[k] for k, other in some]
+    early = early_attention(
+        first_tiles, rows // 2, panel_block, pos, query_latent, q_rope, assemble(arrays_of(first_tiles))
+    )
+    chunks = [
+        late_attention(
+            last_tiles, rows // 2, panel_block, pos, query_latent, q_rope, early, arrays_of(last_tiles), w_uv
+        )
+    ]
+    keys = assemble(arrays_of(tiles))
+    *more, w_out = attention(
+        functools.partial(own_kernel, rows // 2, rows // 2),
+        [rows // 4, rows // 4],
+        panel_block,
+        pos,
+        query_latent,
+        q_rope,
+        w_uv,
+        keys,
+        held=w_out,
+    )
+    chunks += more
+    guests = attention(packed_kernel, [rows // 4, rows // 4], panel_block, packed, w_uk, w_uv, keys)
+
+    blocks = gather_blocks(chunks, {1: guests})
     pieces = []
-    groups = [list(range(row_devices - 1)), [row_devices - 1]]
+    groups = [[[0], list(range(1, last))], [[last]]]
     for group in groups:
-        sent, kept = project([blocks[k] for k in group], w_out, sub_rows)
-        sums = pair_sum(kept, swap(sent, "head", 1))
+        kept, come = [], []
+        for part in group:
+            sent, stays = project([blocks[k] for k in part], w_out, sub_rows)
+            come.append(swap(sent, "head", 1))
+            kept.append(stays)
+        sums = pair_sum(kept, come)
         terms = [sums[0]]
         for j in range(1, len(sums)):
             terms.append(swap(sums[j], "head", 2 * j))
-        for k, total in zip(group, chip_sum(terms)):
+        for k, total in zip(sum(group, []), chip_sum(terms)):
             pieces.append(swap(total, "row", k) if k else total)
     return finish(pieces)
 

time: 110 us -> 94 us (0.85)
  waiting for transfers between devices: 54.3 us -> 30.2 us
  starting transfers between devices: 27.7 us -> 32 us
  Pallas kernels: 26.6 us -> 30.5 us
    ppermute x24 -> x27, waiting for transfers between devices: 54.3 us -> 30.2 us  [swap(): return lax.ppermute(x, axis, [(i, i ^ mask) for i in range(count)])]
    ppermute x24 -> x27, starting transfers between devices: 27.7 us -> 32 us  [swap(): return lax.ppermute(x, axis, [(i, i ^ mask) for i in range(count)])]
    pallas_call x5 -> x8, Pallas kernels: 15.9 us -> 17.9 us  [the longest x2 9.3 us: attention(): pl.pallas_call(kernel, in_specs=[pl.BlockSpec(memory_space=pltpu.SMEM)] +...]
    pallas_call x2 -> x3, Pallas kernels: 5.52 us -> 7.11 us  [project(): pl.pallas_call(functools.partial(project_kernel, sub, len(parts), len(blo...]
    pallas_call x1 -> x2, Pallas kernels: 3.09 us -> 3.26 us  [load(): pl.pallas_call(load_kernel, in_specs=[pl.BlockSpec(memory_space=pltpu.HBM...]
  transfers between devices with their start and end apart: 24 -> 27, of which waited for: 12 -> 10; matrix products, arithmetic and copies ran while one was open for 0% -> 0% of each run, Pallas kernels for 8% -> 31%
where the time goes in v1:
time: 94 us; the launch traced here: 93.7 us
  starting transfers between devices  32 us (34%)
  Pallas kernels  30.5 us (32%)
  waiting for transfers between devices  30.2 us (32%)
    ppermute x27, starting transfers between devices, swap(): return lax.ppermute(x, axis, [(i, i ^ mask) for i in range(count)])  32 us
    ppermute x27, waiting for transfers between devices, swap(): return lax.ppermute(x, axis, [(i, i ^ mask) for i in range(count)])  30.2 us
    pallas_call x2, Pallas kernels, attention(): pl.pallas_call(kernel, in_specs=[pl.BlockSpec(memory_space=pltpu.SMEM)] +...  9.3 us
    pallas_call x3, Pallas kernels, project(): pl.pallas_call(functools.partial(project_kernel, sub, len(parts), len(blo...  7.11 us
    pallas_call x1, Pallas kernels, early_attention(): pl.pallas_call(functools.partial(early_kernel, tiles, rows), in_specs=[pl...  3.53 us
    pallas_call x2, Pallas kernels, load(): pl.pallas_call(load_kernel, in_specs=[pl.BlockSpec(memory_space=pltpu.HBM...  3.26 us
    pallas_call x1, Pallas kernels, late_attention(): pl.pallas_call(functools.partial(late_kernel, tiles, rows), in_specs=[pl....  3.21 us
  transfers between devices with their start and end apart: 27, of which 10 were waited for; matrix products, arithmetic and copies ran while one was open for 0% of the time, Pallas kernels for 31%

profile of v1, /device:TPU:0, one launch (start us, length us, event | category | flops | bytes accessed | tf_op | source)
XLA Modules:
  0.0 93.7 jit_solution(1524522936453058645)
XLA Ops:
  0.0 0.9 panel_half.1.refs_0_
  0.9 4.1 %collective-permute-start.1 = (bf16[576,128]{1,0:T(8,128)(2,1)S(1)}, bf16[576,128]{1,0:T(8,128)(2,1)S(1)}, u32[]{:S(2)}, u32[]{:S(2)}) collective-permute-start(bf16[576,128]{1,0:T(8,128)(2,1)S(1)} %panel_half.1.refs_0_), channel_id=1, source_target_pairs={{0,16},{8,24},{16,0},{24,8},{1,17},{9,25},{17,1},{25,9},{2,18},{10... | collective-permute-start | bytes 442376 | tf_op jit(solution)/shard_map/ppermute | solution.py:27
  5.1 1.6 %collective-permute-start = (bf16[576,128]{1,0:T(8,128)(2,1)S(1)}, bf16[576,128]{1,0:T(8,128)(2,1)S(1)}, u32[]{:S(2)}, u32[]{:S(2)}) collective-permute-start(bf16[576,128]{1,0:T(8,128)(2,1)S(1)} %panel_half.1.refs_0_), channel_id=1, source_target_pairs={{0,8},{8,0},{16,24},{24,16},{1,9},{9,1},{17,25},{25,17},{2,10},{10... | collective-permute-start | bytes 442376 | tf_op jit(solution)/shard_map/ppermute | solution.py:27
  6.6 5.5 %collective-permute-done.1.refs_2_ = bf16[576,128]{1,0:T(8,128)(2,1)S(1)} collective-permute-done((bf16[576,128]{1,0:T(8,128)(2,1)S(1)}, bf16[576,128]{1,0:T(8,128)(2,1)S(1)}, u32[]{:S(2)}, u32[]{:S(2)}) %collective-permute-start.1) | collective-permute-done | bytes 147488 | tf_op jit(solution)/shard_map/ppermute | solution.py:27
  12.2 0.6 collective-permute-start.5
  12.8 0.5 collective-permute-start.4
  13.3 0.0 collective-permute-done.refs_1_
  13.3 0.0 collective-permute-start.3
  13.3 0.7 copy-done.2
  14.0 1.0 %pack.1 = bf16[64,3200]{1,0:T(8,128)(2,1)S(1)} custom-call(s32[1,128]{1,0:T(1,128)S(1)} %bitcast.1, bf16[128,2048]{1,0:T(8,128)(2,1)} %nope_ref.3, bf16[128,1024]{1,0:T(8,128)(2,1)} %rope_ref.9), custom_call_target="tpu_custom_call" | custom-call | flops 1000000 | bytes 409600 | tf_op jit(solution)/shard_map/pack/pallas_call | solution.py:154
  15.0 1.5 %collective-permute-start.8 = (bf16[64,3200]{1,0:T(8,128)(2,1)S(1)}, bf16[64,3200]{1,0:T(8,128)(2,1)S(1)}, u32[]{:S(2)}, u32[]{:S(2)}) collective-permute-start(bf16[64,3200]{1,0:T(8,128)(2,1)S(1)} %pack.1), channel_id=1, source_target_pairs={{0,8},{8,0},{16,24},{24,16},{1,9},{9,1},{17,25},{25,17},{2,10},{10... | collective-permute-start | bytes 1228808 | tf_op jit(solution)/shard_map/ppermute | solution.py:27
  16.4 1.6 %load.3.rest_2_.up_ref = bf16[16,512,128]{2,1,0:T(8,128)(2,1)S(1)} custom-call(bf16[16,512,128]{2,1,0:T(8,128)(2,1)} %hbm_ref.3), custom_call_target="tpu_custom_call" | custom-call | flops 4000000 | bytes 2097152 | tf_op jit(solution)/shard_map/load/pallas_call | solution.py:81
  18.1 0.0 copy-start.1
  18.1 1.7 %load.2.absorb_ref = bf16[16,128,512]{2,1,0:T(8,128)(2,1)S(1)} custom-call(bf16[16,128,512]{2,1,0:T(8,128)(2,1)} %hbm_ref.2), custom_call_target="tpu_custom_call" | custom-call | flops 4000000 | bytes 2097152 | tf_op jit(solution)/shard_map/load/pallas_call | solution.py:81
  19.7 0.0 copy-start
  19.8 0.0 copy-start.3
  19.8 0.0 copy-start.4
  19.8 0.7 queries.1.latent_ref
  20.5 0.3 collective-permute-start.6
  20.8 0.0 collective-permute-done.2.refs_3_.refs_4_
  20.8 0.0 collective-permute-done.4.refs_5_.refs_6_
  20.8 0.0 collective-permute-done.3.refs_4_.refs_5_
  20.8 0.2 assemble.2.keys_ref
  21.0 3.5 %early_attention.1 = (f32[1024,1]{1,0:T(8,128)S(1)}, f32[1024,1]{1,0:T(8,128)S(1)}, f32[1024,512]{1,0:T(8,128)S(1)}) custom-call(s32[4]{0:T(128)S(1)} %copy-done.4, s32[1,128]{1,0:T(1,128)S(1)} %bitcast.2, bf16[16,128,512]{2,1,0:T(8,128)(2,1)S(1)} %queries.1.latent_ref, bf16[128,1024]{1,0:T(8,128)(2,1)S(1)} %copy-done, bf16[576,768]{1,0:T(8,128)(2,1)S(1)} %assemble.2.keys_ref), custom_call_target="tpu_custom_call" | custom-call | flops 1711276032 | bytes 4194304 | tf_op jit(solution)/shard_map/early_attention/pallas_call | solution.py:307
  24.5 0.0 collective-permute-done.6.rest_1_.refs_7_
  24.5 3.2 %late_attention.1.refs_0_ = bf16[64,2048]{1,0:T(8,128)(2,1)S(1)} custom-call(s32[4]{0:T(128)S(1)} %copy-done.4, s32[1,128]{1,0:T(1,128)S(1)} %bitcast.3, bf16[16,128,512]{2,1,0:T(8,128)(2,1)S(1)} %queries.1.latent_ref, bf16[128,1024]{1,0:T(8,128)(2,1)S(1)} %copy-done, f32[1024,1]{1,0:T(8,128)S(1)} %get-tuple-element.30.top_ref, ...), custom_call_target="tpu_custom_call" | custom-call | flops 704643072 | bytes 4194304 | tf_op jit(solution)/shard_map/late_attention/pallas_call | solution.py:327
  27.8 2.3 %collective-permute-start.9 = (bf16[64,2048]{1,0:T(8,128)(2,1)S(1)}, bf16[64,2048]{1,0:T(8,128)(2,1)S(1)}, u32[]{:S(2)}, u32[]{:S(2)}) collective-permute-start(bf16[64,2048]{1,0:T(8,128)(2,1)S(1)} %late_attention.1.refs_0_), channel_id=1, source_target_pairs={{0,16},{8,24},{16,0},{24,8},{1,17},{9,25},{17,1},{25,9},{2,18},{10... | collective-permute-start | bytes 786440 | tf_op jit(solution)/shard_map/ppermute | solution.py:27
  30.1 1.7 %collective-permute-start.7 = (bf16[64,2048]{1,0:T(8,128)(2,1)S(1)}, bf16[64,2048]{1,0:T(8,128)(2,1)S(1)}, u32[]{:S(2)}, u32[]{:S(2)}) collective-permute-start(bf16[64,2048]{1,0:T(8,128)(2,1)S(1)} %late_attention.1.refs_0_), channel_id=1, source_target_pairs={{0,8},{8,0},{16,24},{24,16},{1,9},{9,1},{17,25},{25,17},{2,10},{10... | collective-permute-start | bytes 786440 | tf_op jit(solution)/shard_map/ppermute | solution.py:27
  31.8 0.3 assemble.3.keys_ref
  32.2 4.4 %attention.2 = (bf16[32,2048]{1,0:T(8,128)(2,1)S(1)}, bf16[32,2048]{1,0:T(8,128)(2,1)S(1)}, bf16[1792,2048]{1,0:T(8,128)(2,1)S(1)}) custom-call(s32[4]{0:T(128)S(1)} %copy-done.4, s32[1,128]{1,0:T(1,128)S(1)} %bitcast.4, bf16[16,128,512]{2,1,0:T(8,128)(2,1)S(1)} %queries.1.latent_ref, bf16[128,1024]{1,0:T(8,128)(2,1)S(1)} %copy-done, ...), custom_call_target="tpu_custom_call" | custom-call | flops 2415919104 | bytes 8388608 | tf_op jit(solution)/shard_map/attention/pallas_call | solution.py:391
  36.6 0.2 collective-permute-start.10
  36.7 2.8 %collective-permute-start.11 = (bf16[32,2048]{1,0:T(8,128)(2,1)S(1)}, bf16[32,2048]{1,0:T(8,128)(2,1)S(1)}, u32[]{:S(2)}, u32[]{:S(2)}) collective-permute-start(bf16[32,2048]{1,0:T(8,128)(2,1)S(1)} %get-tuple-element.34.refs_2_), channel_id=1, source_target_pairs={{0,16},{8,24},{16,0},{24,8},{1,17},{9,25},{17,1},{25,9},{2,18},{10... | collective-permute-start | bytes 393224 | tf_op jit(solution)/shard_map/ppermute | solution.py:27
  39.6 4.9 %attention.3 = (bf16[32,2048]{1,0:T(8,128)(2,1)S(1)}, bf16[32,2048]{1,0:T(8,128)(2,1)S(1)}) custom-call(s32[4]{0:T(128)S(1)} %copy-done.4, bf16[64,3200]{1,0:T(8,128)(2,1)S(1)} %collective-permute-done.8.packed_ref, bf16[16,128,512]{2,1,0:T(8,128)(2,1)S(1)} %load.2.absorb_ref, bf16[16,512,128]{2,1,0:T(8,128)(2,1)S(1)} %load.3.rest_2_.up_ref, ...), custom_call_target="tpu_custom_call" | custom-call | flops 2415919104 | bytes 8388608 | tf_op jit(solution)/shard_map/attention/pallas_call | solution.py:391
  44.5 0.0 collective-permute-done.9.refs_3_
  44.5 0.4 collective-permute-start.19
  44.9 7.2 %collective-permute-done.10.refs_4_ = bf16[32,2048]{1,0:T(8,128)(2,1)S(1)} collective-permute-done((bf16[32,2048]{1,0:T(8,128)(2,1)S(1)}, bf16[32,2048]{1,0:T(8,128)(2,1)S(1)}, u32[]{:S(2)}, u32[]{:S(2)}) %collective-permute-start.10) | collective-permute-done | bytes 131104 | tf_op jit(solution)/shard_map/ppermute | solution.py:27
  52.1 2.1 %collective-permute-done.11.refs_5_ = bf16[32,2048]{1,0:T(8,128)(2,1)S(1)} collective-permute-done((bf16[32,2048]{1,0:T(8,128)(2,1)S(1)}, bf16[32,2048]{1,0:T(8,128)(2,1)S(1)}, u32[]{:S(2)}, u32[]{:S(2)}) %collective-permute-start.11) | collective-permute-done | bytes 131104 | tf_op jit(solution)/shard_map/ppermute | solution.py:27
  54.2 2.1 %project.4 = (bf16[2,4,16,1792]{3,2,1,0:T(8,128)(2,1)S(1)}, f32[2,4,16,1792]{3,2,1,0:T(8,128)S(1)}) custom-call(bf16[64,2048]{1,0:T(8,128)(2,1)S(1)} %collective-permute-done.7.refs_0_, bf16[32,2048]{1,0:T(8,128)(2,1)S(1)} %get-tuple-element.37.refs_1_, bf16[32,2048]{1,0:T(8,128)(2,1)S(1)} %get-tuple-element.38.refs_2_, ...), custom_call_target="tpu_custom_call" | custom-call | flops 1879048192 | bytes 7864320 | tf_op jit(solution)/shard_map/project/pallas_call | solution.py:429
  56.4 0.1 collective-permute-start.13
  56.4 0.1 collective-permute-start.20
  56.5 2.0 %collective-permute-start.21 = (bf16[32,2048]{1,0:T(8,128)(2,1)S(1)}, bf16[32,2048]{1,0:T(8,128)(2,1)S(1)}, u32[]{:S(2)}, u32[]{:S(2)}) collective-permute-start(bf16[32,2048]{1,0:T(8,128)(2,1)S(1)} %collective-permute-done.11.refs_5_), channel_id=1, source_target_pairs={{0,8},{8,0},{16,24},{24,16},{1,9},{9,1},{17,25},{25,17},{2,10},{10... | collective-permute-start | bytes 393224 | tf_op jit(solution)/shard_map/ppermute | solution.py:27
  58.5 2.5 %project.3 = (bf16[1,4,16,1792]{3,2,1,0:T(8,128)(2,1)S(1)}, f32[1,4,16,1792]{3,2,1,0:T(8,128)S(1)}) custom-call(bf16[64,2048]{1,0:T(8,128)(2,1)S(1)} %late_attention.1.refs_0_, bf16[32,2048]{1,0:T(8,128)(2,1)S(1)} %get-tuple-element.33.refs_1_, bf16[32,2048]{1,0:T(8,128)(2,1)S(1)} %get-tuple-element.34.refs_2_, ...), custom_call_target="tpu_custom_call" | custom-call | flops 939524096 | bytes 7864320 | tf_op jit(solution)/shard_map/project/pallas_call | solution.py:429
  61.0 0.1 collective-permute-start.12
  61.1 1.8 %collective-permute-done.20.refs_1_ = bf16[32,2048]{1,0:T(8,128)(2,1)S(1)} collective-permute-done((bf16[32,2048]{1,0:T(8,128)(2,1)S(1)}, bf16[32,2048]{1,0:T(8,128)(2,1)S(1)}, u32[]{:S(2)}, u32[]{:S(2)}) %collective-permute-start.20) | collective-permute-done | bytes 131104 | tf_op jit(solution)/shard_map/ppermute | solution.py:27
  62.9 2.3 %collective-permute-done.21.refs_2_ = bf16[32,2048]{1,0:T(8,128)(2,1)S(1)} collective-permute-done((bf16[32,2048]{1,0:T(8,128)(2,1)S(1)}, bf16[32,2048]{1,0:T(8,128)(2,1)S(1)}, u32[]{:S(2)}, u32[]{:S(2)}) %collective-permute-start.21) | collective-permute-done | bytes 131104 | tf_op jit(solution)/shard_map/ppermute | solution.py:27
  65.2 2.5 %project.5 = (bf16[1,4,16,1792]{3,2,1,0:T(8,128)(2,1)S(1)}, f32[1,4,16,1792]{3,2,1,0:T(8,128)S(1)}) custom-call(bf16[64,2048]{1,0:T(8,128)(2,1)S(1)} %collective-permute-done.19.refs_0_, bf16[32,2048]{1,0:T(8,128)(2,1)S(1)} %collective-permute-done.20.refs_1_, bf16[32,2048]{1,0:T(8,128)(2,1)S(1)} %collective-permute-done.21.refs_2_, ...), custom_call_target="tpu_custom_call" | custom-call | flops 939524096 | bytes 7864320 | tf_op jit(solution)/shard_map/project/pallas_call | solution.py:429
  67.6 0.1 collective-permute-start.22
  67.7 0.1 pair_sum.2
  67.9 1.6 %collective-permute-start.14 = (bf16[3,16,1792]{2,1,0:T(8,128)(2,1)S(1)}, bf16[3,16,1792]{2,1,0:T(8,128)(2,1)S(1)}, u32[]{:S(2)}, u32[]{:S(2)}) collective-permute-start(bf16[3,16,1792]{2,1,0:T(8,128)(2,1)S(1)} %get-tuple-element.43), channel_id=1, source_target_pairs={{0,2},{1,3},{2,0},{3,1},{4,6},{5,7},{6,4},{7,5},{8,10},{9,11},{10,... | collective-permute-start | bytes 516104 | tf_op jit(solution)/shard_map/ppermute | solution.py:27
  69.5 1.5 %collective-permute-start.15 = (bf16[3,16,1792]{2,1,0:T(8,128)(2,1)S(1)}, bf16[3,16,1792]{2,1,0:T(8,128)(2,1)S(1)}, u32[]{:S(2)}, u32[]{:S(2)}) collective-permute-start(bf16[3,16,1792]{2,1,0:T(8,128)(2,1)S(1)} %get-tuple-element.44), channel_id=1, source_target_pairs={{0,4},{1,5},{2,6},{3,7},{4,0},{5,1},{6,2},{7,3},{8,12},{9,13},{10,... | collective-permute-start | bytes 516104 | tf_op jit(solution)/shard_map/ppermute | solution.py:27
  71.0 0.4 collective-permute-start.16
  71.5 1.6 %collective-permute-start.23 = (bf16[1,16,1792]{2,1,0:T(8,128)(2,1)S(1)}, bf16[1,16,1792]{2,1,0:T(8,128)(2,1)S(1)}, u32[]{:S(2)}, u32[]{:S(2)}) collective-permute-start(bf16[1,16,1792]{2,1,0:T(8,128)(2,1)S(1)} %get-tuple-element.52), channel_id=1, source_target_pairs={{0,2},{1,3},{2,0},{3,1},{4,6},{5,7},{6,4},{7,5},{8,10},{9,11},{10,... | collective-permute-start | bytes 172040 | tf_op jit(solution)/shard_map/ppermute | solution.py:27
  73.1 1.5 %collective-permute-start.24 = (bf16[1,16,1792]{2,1,0:T(8,128)(2,1)S(1)}, bf16[1,16,1792]{2,1,0:T(8,128)(2,1)S(1)}, u32[]{:S(2)}, u32[]{:S(2)}) collective-permute-start(bf16[1,16,1792]{2,1,0:T(8,128)(2,1)S(1)} %get-tuple-element.53), channel_id=1, source_target_pairs={{0,4},{1,5},{2,6},{3,7},{4,0},{5,1},{6,2},{7,3},{8,12},{9,13},{10,... | collective-permute-start | bytes 172040 | tf_op jit(solution)/shard_map/ppermute | solution.py:27
  74.6 5.1 %collective-permute-done.23.refs_1_ = bf16[1,16,1792]{2,1,0:T(8,128)(2,1)S(1)} collective-permute-done((bf16[1,16,1792]{2,1,0:T(8,128)(2,1)S(1)}, bf16[1,16,1792]{2,1,0:T(8,128)(2,1)S(1)}, u32[]{:S(2)}, u32[]{:S(2)}) %collective-permute-start.23) | collective-permute-done | bytes 57376 | tf_op jit(solution)/shard_map/ppermute | solution.py:27
  79.7 2.5 %collective-permute-start.25 = (bf16[1,16,1792]{2,1,0:T(8,128)(2,1)S(1)}, bf16[1,16,1792]{2,1,0:T(8,128)(2,1)S(1)}, u32[]{:S(2)}, u32[]{:S(2)}) collective-permute-start(bf16[1,16,1792]{2,1,0:T(8,128)(2,1)S(1)} %get-tuple-element.54), channel_id=1, source_target_pairs={{0,6},{1,7},{2,4},{3,5},{4,2},{5,3},{6,0},{7,1},{8,14},{9,15},{10,... | collective-permute-start | bytes 172040 | tf_op jit(solution)/shard_map/ppermute | solution.py:27
  82.2 2.6 %collective-permute-done.25.refs_3_ = bf16[1,16,1792]{2,1,0:T(8,128)(2,1)S(1)} collective-permute-done((bf16[1,16,1792]{2,1,0:T(8,128)(2,1)S(1)}, bf16[1,16,1792]{2,1,0:T(8,128)(2,1)S(1)}, u32[]{:S(2)}, u32[]{:S(2)}) %collective-permute-start.25) | collective-permute-done | bytes 57376 | tf_op jit(solution)/shard_map/ppermute | solution.py:27
  84.8 2.9 %collective-permute-start.26 = (bf16[16,1792]{1,0:T(8,128)(2,1)S(1)}, bf16[16,1792]{1,0:T(8,128)(2,1)S(1)}, u32[]{:S(2)}, u32[]{:S(2)}) collective-permute-start(bf16[16,1792]{1,0:T(8,128)(2,1)S(1)} %chip_sum.3), channel_id=1, source_target_pairs={{0,24},{8,16},{16,8},{24,0},{1,25},{9,17},{17,9},{25,1},{2,26},{10... | collective-permute-start | bytes 172040 | tf_op jit(solution)/shard_map/ppermute | solution.py:27
  87.7 0.1 chip_sum.2
  87.8 0.1 collective-permute-start.17
  87.9 1.5 %collective-permute-start.18 = (bf16[16,1792]{1,0:T(8,128)(2,1)S(1)}, bf16[16,1792]{1,0:T(8,128)(2,1)S(1)}, u32[]{:S(2)}, u32[]{:S(2)}) collective-permute-start(bf16[16,1792]{1,0:T(8,128)(2,1)S(1)} %get-tuple-element.48), channel_id=1, source_target_pairs={{0,16},{8,24},{16,0},{24,8},{1,17},{9,25},{17,1},{25,9},{2,18},{10... | collective-permute-start | bytes 172040 | tf_op jit(solution)/shard_map/ppermute | solution.py:27
  89.4 1.5 %collective-permute-done.26.refs_3_ = bf16[16,1792]{1,0:T(8,128)(2,1)S(1)} collective-permute-done((bf16[16,1792]{1,0:T(8,128)(2,1)S(1)}, bf16[16,1792]{1,0:T(8,128)(2,1)S(1)}, u32[]{:S(2)}, u32[]{:S(2)}) %collective-permute-start.26) | collective-permute-done | bytes 57376 | tf_op jit(solution)/shard_map/ppermute | solution.py:27
  90.9 1.1 %collective-permute-done.17.refs_1_ = bf16[16,1792]{1,0:T(8,128)(2,1)S(1)} collective-permute-done((bf16[16,1792]{1,0:T(8,128)(2,1)S(1)}, bf16[16,1792]{1,0:T(8,128)(2,1)S(1)}, u32[]{:S(2)}, u32[]{:S(2)}) %collective-permute-start.17) | collective-permute-done | bytes 57376 | tf_op jit(solution)/shard_map/ppermute | solution.py:27
  92.0 1.0 %collective-permute-done.18.refs_2_ = bf16[16,1792]{1,0:T(8,128)(2,1)S(1)} collective-permute-done((bf16[16,1792]{1,0:T(8,128)(2,1)S(1)}, bf16[16,1792]{1,0:T(8,128)(2,1)S(1)}, u32[]{:S(2)}, u32[]{:S(2)}) %collective-permute-start.18) | collective-permute-done | bytes 57376 | tf_op jit(solution)/shard_map/ppermute | solution.py:27
  93.0 0.7 finish.1
  (19 shorter events, 0.1 us)
Async XLA Ops:
  0.9 11.2 %collective-permute-start.1 = (bf16[576,128]{1,0:T(8,128)(2,1)S(1)}, bf16[576,128]{1,0:T(8,128)(2,1)S(1)}, u32[]{:S(2)}, u32[]{:S(2)}) collective-permute-start(bf16[576,128]{1,0:T(8,128)(2,1)S(1)} %panel_half.1.refs_0_), channel_id=1, source_target_pairs={{0,16},{8,24},{16,0},{24,8},{1,17},{9,25},{17,1},{25,9},{2,18},{10... | collective-permute-start | bytes 442376 | tf_op jit(solution)/shard_map/ppermute | solution.py:27
  5.1 8.2 %collective-permute-start = (bf16[576,128]{1,0:T(8,128)(2,1)S(1)}, bf16[576,128]{1,0:T(8,128)(2,1)S(1)}, u32[]{:S(2)}, u32[]{:S(2)}) collective-permute-start(bf16[576,128]{1,0:T(8,128)(2,1)S(1)} %panel_half.1.refs_0_), channel_id=1, source_target_pairs={{0,8},{8,0},{16,24},{24,16},{1,9},{9,1},{17,25},{25,17},{2,10},{10... | collective-permute-start | bytes 442376 | tf_op jit(solution)/shard_map/ppermute | solution.py:27
  12.2 8.3 %collective-permute-start.5 = (bf16[576,128]{1,0:T(8,128)(2,1)S(1)}, bf16[576,128]{1,0:T(8,128)(2,1)S(1)}, u32[]{:S(2)}, u32[]{:S(2)}) collective-permute-start(bf16[576,128]{1,0:T(8,128)(2,1)S(1)} %collective-permute-done.1.refs_2_), channel_id=1, source_target_pairs={{0,8},{8,0},{16,24},{24,16},{1,9},{9,1},{17,25},{25,17},{2,10},{10... | collective-permute-start | bytes 442376 | tf_op jit(solution)/shard_map/ppermute | solution.py:27
  12.8 8.0 %collective-permute-start.2 = (bf16[576,128]{1,0:T(8,128)(2,1)S(1)}, bf16[576,128]{1,0:T(8,128)(2,1)S(1)}, u32[]{:S(2)}, u32[]{:S(2)}) collective-permute-start(bf16[576,128]{1,0:T(8,128)(2,1)S(1)} %panel_half.1.refs_0_), channel_id=1, source_target_pairs={{0,1},{1,0},{2,3},{3,2},{4,5},{5,4},{6,7},{7,6},{8,9},{9,8},{10,11... | collective-permute-start | bytes 442376 | tf_op jit(solution)/shard_map/ppermute | solution.py:27
  12.8 8.0 %collective-permute-start.4 = (bf16[576,128]{1,0:T(8,128)(2,1)S(1)}, bf16[576,128]{1,0:T(8,128)(2,1)S(1)}, u32[]{:S(2)}, u32[]{:S(2)}) collective-permute-start(bf16[576,128]{1,0:T(8,128)(2,1)S(1)} %collective-permute-done.1.refs_2_), channel_id=1, source_target_pairs={{0,1},{1,0},{2,3},{3,2},{4,5},{5,4},{6,7},{7,6},{8,9},{9,8},{10,11... | collective-permute-start | bytes 442376 | tf_op jit(solution)/shard_map/ppermute | solution.py:27
  13.3 7.5 %collective-permute-start.3 = (bf16[576,128]{1,0:T(8,128)(2,1)S(1)}, bf16[576,128]{1,0:T(8,128)(2,1)S(1)}, u32[]{:S(2)}, u32[]{:S(2)}) collective-permute-start(bf16[576,128]{1,0:T(8,128)(2,1)S(1)} %collective-permute-done.refs_1_), channel_id=1, source_target_pairs={{0,1},{1,0},{2,3},{3,2},{4,5},{5,4},{6,7},{7,6},{8,9},{9,8},{10,11... | collective-permute-start | bytes 442376 | tf_op jit(solution)/shard_map/ppermute | solution.py:27
  13.3 0.7 copy-start.2
  15.0 24.6 %collective-permute-start.8 = (bf16[64,3200]{1,0:T(8,128)(2,1)S(1)}, bf16[64,3200]{1,0:T(8,128)(2,1)S(1)}, u32[]{:S(2)}, u32[]{:S(2)}) collective-permute-start(bf16[64,3200]{1,0:T(8,128)(2,1)S(1)} %pack.1), channel_id=1, source_target_pairs={{0,8},{8,0},{16,24},{24,16},{1,9},{9,1},{17,25},{25,17},{2,10},{10... | collective-permute-start | bytes 1228808 | tf_op jit(solution)/shard_map/ppermute | solution.py:27
  18.1 1.7 %copy-start.1 = (bf16[128,2048]{1,0:T(8,128)(2,1)S(1)}, bf16[128,2048]{1,0:T(8,128)(2,1)}, u32[]{:S(2)}) copy-start(bf16[128,2048]{1,0:T(8,128)(2,1)} %nope_ref.3) | copy-start | bytes 1572868
  19.7 1.2 %copy-start = (bf16[128,1024]{1,0:T(8,128)(2,1)S(1)}, bf16[128,1024]{1,0:T(8,128)(2,1)}, u32[]{:S(2)}) copy-start(bf16[128,1024]{1,0:T(8,128)(2,1)} %rope_ref.9) | copy-start | bytes 786436
  19.8 1.2 %copy-start.3 = (s32[128]{0:T(128)S(1)}, s32[128]{0:T(128)}, u32[]{:S(2)}) copy-start(s32[128]{0:T(128)} %param.14) | copy-start | bytes 1540
  19.8 1.2 %copy-start.4 = (s32[4]{0:T(128)S(1)}, s32[4]{0:T(128)}, u32[]{:S(2)}) copy-start(s32[4]{0:T(128)} %block_ref.7) | copy-start | bytes 52
  20.5 4.0 %collective-permute-start.6 = (bf16[576,128]{1,0:T(8,128)(2,1)S(1)}, bf16[576,128]{1,0:T(8,128)(2,1)S(1)}, u32[]{:S(2)}, u32[]{:S(2)}) collective-permute-start(bf16[576,128]{1,0:T(8,128)(2,1)S(1)} %collective-permute-done.5.rest_0_.refs_3_), channel_id=1, source_target_pairs={{0,1},{1,0},{2,3},{3,2},{4,5},{5,4},{6,7},{7,6},{8,9},{9,8},{10,11... | collective-permute-start | bytes 442376 | tf_op jit(solution)/shard_map/ppermute | solution.py:27
  27.8 16.7 %collective-permute-start.9 = (bf16[64,2048]{1,0:T(8,128)(2,1)S(1)}, bf16[64,2048]{1,0:T(8,128)(2,1)S(1)}, u32[]{:S(2)}, u32[]{:S(2)}) collective-permute-start(bf16[64,2048]{1,0:T(8,128)(2,1)S(1)} %late_attention.1.refs_0_), channel_id=1, source_target_pairs={{0,16},{8,24},{16,0},{24,8},{1,17},{9,25},{17,1},{25,9},{2,18},{10... | collective-permute-start | bytes 786440 | tf_op jit(solution)/shard_map/ppermute | solution.py:27
  30.1 24.1 %collective-permute-start.7 = (bf16[64,2048]{1,0:T(8,128)(2,1)S(1)}, bf16[64,2048]{1,0:T(8,128)(2,1)S(1)}, u32[]{:S(2)}, u32[]{:S(2)}) collective-permute-start(bf16[64,2048]{1,0:T(8,128)(2,1)S(1)} %late_attention.1.refs_0_), channel_id=1, source_target_pairs={{0,8},{8,0},{16,24},{24,16},{1,9},{9,1},{17,25},{25,17},{2,10},{10... | collective-permute-start | bytes 786440 | tf_op jit(solution)/shard_map/ppermute | solution.py:27
  36.6 15.5 %collective-permute-start.10 = (bf16[32,2048]{1,0:T(8,128)(2,1)S(1)}, bf16[32,2048]{1,0:T(8,128)(2,1)S(1)}, u32[]{:S(2)}, u32[]{:S(2)}) collective-permute-start(bf16[32,2048]{1,0:T(8,128)(2,1)S(1)} %get-tuple-element.33.refs_1_), channel_id=1, source_target_pairs={{0,16},{8,24},{16,0},{24,8},{1,17},{9,25},{17,1},{25,9},{2,18},{10... | collective-permute-start | bytes 393224 | tf_op jit(solution)/shard_map/ppermute | solution.py:27
  36.7 17.5 %collective-permute-start.11 = (bf16[32,2048]{1,0:T(8,128)(2,1)S(1)}, bf16[32,2048]{1,0:T(8,128)(2,1)S(1)}, u32[]{:S(2)}, u32[]{:S(2)}) collective-permute-start(bf16[32,2048]{1,0:T(8,128)(2,1)S(1)} %get-tuple-element.34.refs_2_), channel_id=1, source_target_pairs={{0,16},{8,24},{16,0},{24,8},{1,17},{9,25},{17,1},{25,9},{2,18},{10... | collective-permute-start | bytes 393224 | tf_op jit(solution)/shard_map/ppermute | solution.py:27
  44.5 20.7 %collective-permute-start.19 = (bf16[64,2048]{1,0:T(8,128)(2,1)S(1)}, bf16[64,2048]{1,0:T(8,128)(2,1)S(1)}, u32[]{:S(2)}, u32[]{:S(2)}) collective-permute-start(bf16[64,2048]{1,0:T(8,128)(2,1)S(1)} %collective-permute-done.9.refs_3_), channel_id=1, source_target_pairs={{0,8},{8,0},{16,24},{24,16},{1,9},{9,1},{17,25},{25,17},{2,10},{10... | collective-permute-start | bytes 786440 | tf_op jit(solution)/shard_map/ppermute | solution.py:27
  56.4 11.4 %collective-permute-start.13 = (bf16[2,4,16,1792]{3,2,1,0:T(8,128)(2,1)S(1)}, bf16[2,4,16,1792]{3,2,1,0:T(8,128)(2,1)S(1)}, u32[]{:S(2)}, u32[]{:S(2)}) collective-permute-start(bf16[2,4,16,1792]{3,2,1,0:T(8,128)(2,1)S(1)} %get-tuple-element.41), channel_id=1, source_target_pairs={{0,1},{1,0},{2,3},{3,2},{4,5},{5,4},{6,7},{7,6},{8,9},{9,8},{10,11... | collective-permute-start | bytes 1376264 | tf_op jit(solution)/shard_map/ppermute | solution.py:27
  56.4 6.4 %collective-permute-start.20 = (bf16[32,2048]{1,0:T(8,128)(2,1)S(1)}, bf16[32,2048]{1,0:T(8,128)(2,1)S(1)}, u32[]{:S(2)}, u32[]{:S(2)}) collective-permute-start(bf16[32,2048]{1,0:T(8,128)(2,1)S(1)} %collective-permute-done.10.refs_4_), channel_id=1, source_target_pairs={{0,8},{8,0},{16,24},{24,16},{1,9},{9,1},{17,25},{25,17},{2,10},{10... | collective-permute-start | bytes 393224 | tf_op jit(solution)/shard_map/ppermute | solution.py:27
  56.5 8.6 %collective-permute-start.21 = (bf16[32,2048]{1,0:T(8,128)(2,1)S(1)}, bf16[32,2048]{1,0:T(8,128)(2,1)S(1)}, u32[]{:S(2)}, u32[]{:S(2)}) collective-permute-start(bf16[32,2048]{1,0:T(8,128)(2,1)S(1)} %collective-permute-done.11.refs_5_), channel_id=1, source_target_pairs={{0,8},{8,0},{16,24},{24,16},{1,9},{9,1},{17,25},{25,17},{2,10},{10... | collective-permute-start | bytes 393224 | tf_op jit(solution)/shard_map/ppermute | solution.py:27
  61.0 6.7 %collective-permute-start.12 = (bf16[1,4,16,1792]{3,2,1,0:T(8,128)(2,1)S(1)}, bf16[1,4,16,1792]{3,2,1,0:T(8,128)(2,1)S(1)}, u32[]{:S(2)}, u32[]{:S(2)}) collective-permute-start(bf16[1,4,16,1792]{3,2,1,0:T(8,128)(2,1)S(1)} %get-tuple-element.40), channel_id=1, source_target_pairs={{0,1},{1,0},{2,3},{3,2},{4,5},{5,4},{6,7},{7,6},{8,9},{9,8},{10,11... | collective-permute-start | bytes 688136 | tf_op jit(solution)/shard_map/ppermute | solution.py:27
  67.6 3.8 %collective-permute-start.22 = (bf16[1,4,16,1792]{3,2,1,0:T(8,128)(2,1)S(1)}, bf16[1,4,16,1792]{3,2,1,0:T(8,128)(2,1)S(1)}, u32[]{:S(2)}, u32[]{:S(2)}) collective-permute-start(bf16[1,4,16,1792]{3,2,1,0:T(8,128)(2,1)S(1)} %get-tuple-element.50), channel_id=1, source_target_pairs={{0,1},{1,0},{2,3},{3,2},{4,5},{5,4},{6,7},{7,6},{8,9},{9,8},{10,11... | collective-permute-start | bytes 688136 | tf_op jit(solution)/shard_map/ppermute | solution.py:27
  67.9 19.8 %collective-permute-start.14 = (bf16[3,16,1792]{2,1,0:T(8,128)(2,1)S(1)}, bf16[3,16,1792]{2,1,0:T(8,128)(2,1)S(1)}, u32[]{:S(2)}, u32[]{:S(2)}) collective-permute-start(bf16[3,16,1792]{2,1,0:T(8,128)(2,1)S(1)} %get-tuple-element.43), channel_id=1, source_target_pairs={{0,2},{1,3},{2,0},{3,1},{4,6},{5,7},{6,4},{7,5},{8,10},{9,11},{10,... | collective-permute-start | bytes 516104 | tf_op jit(solution)/shard_map/ppermute | solution.py:27
  69.5 18.2 %collective-permute-start.15 = (bf16[3,16,1792]{2,1,0:T(8,128)(2,1)S(1)}, bf16[3,16,1792]{2,1,0:T(8,128)(2,1)S(1)}, u32[]{:S(2)}, u32[]{:S(2)}) collective-permute-start(bf16[3,16,1792]{2,1,0:T(8,128)(2,1)S(1)} %get-tuple-element.44), channel_id=1, source_target_pairs={{0,4},{1,5},{2,6},{3,7},{4,0},{5,1},{6,2},{7,3},{8,12},{9,13},{10,... | collective-permute-start | bytes 516104 | tf_op jit(solution)/shard_map/ppermute | solution.py:27
  71.0 16.7 %collective-permute-start.16 = (bf16[3,16,1792]{2,1,0:T(8,128)(2,1)S(1)}, bf16[3,16,1792]{2,1,0:T(8,128)(2,1)S(1)}, u32[]{:S(2)}, u32[]{:S(2)}) collective-permute-start(bf16[3,16,1792]{2,1,0:T(8,128)(2,1)S(1)} %get-tuple-element.45), channel_id=1, source_target_pairs={{0,6},{1,7},{2,4},{3,5},{4,2},{5,3},{6,0},{7,1},{8,14},{9,15},{10,... | collective-permute-start | bytes 516104 | tf_op jit(solution)/shard_map/ppermute | solution.py:27
  71.5 8.2 %collective-permute-start.23 = (bf16[1,16,1792]{2,1,0:T(8,128)(2,1)S(1)}, bf16[1,16,1792]{2,1,0:T(8,128)(2,1)S(1)}, u32[]{:S(2)}, u32[]{:S(2)}) collective-permute-start(bf16[1,16,1792]{2,1,0:T(8,128)(2,1)S(1)} %get-tuple-element.52), channel_id=1, source_target_pairs={{0,2},{1,3},{2,0},{3,1},{4,6},{5,7},{6,4},{7,5},{8,10},{9,11},{10,... | collective-permute-start | bytes 172040 | tf_op jit(solution)/shard_map/ppermute | solution.py:27
  73.1 9.1 %collective-permute-start.24 = (bf16[1,16,1792]{2,1,0:T(8,128)(2,1)S(1)}, bf16[1,16,1792]{2,1,0:T(8,128)(2,1)S(1)}, u32[]{:S(2)}, u32[]{:S(2)}) collective-permute-start(bf16[1,16,1792]{2,1,0:T(8,128)(2,1)S(1)} %get-tuple-element.53), channel_id=1, source_target_pairs={{0,4},{1,5},{2,6},{3,7},{4,0},{5,1},{6,2},{7,3},{8,12},{9,13},{10,... | collective-permute-start | bytes 172040 | tf_op jit(solution)/shard_map/ppermute | solution.py:27
  79.7 5.1 %collective-permute-start.25 = (bf16[1,16,1792]{2,1,0:T(8,128)(2,1)S(1)}, bf16[1,16,1792]{2,1,0:T(8,128)(2,1)S(1)}, u32[]{:S(2)}, u32[]{:S(2)}) collective-permute-start(bf16[1,16,1792]{2,1,0:T(8,128)(2,1)S(1)} %get-tuple-element.54), channel_id=1, source_target_pairs={{0,6},{1,7},{2,4},{3,5},{4,2},{5,3},{6,0},{7,1},{8,14},{9,15},{10,... | collective-permute-start | bytes 172040 | tf_op jit(solution)/shard_map/ppermute | solution.py:27
  84.8 6.2 %collective-permute-start.26 = (bf16[16,1792]{1,0:T(8,128)(2,1)S(1)}, bf16[16,1792]{1,0:T(8,128)(2,1)S(1)}, u32[]{:S(2)}, u32[]{:S(2)}) collective-permute-start(bf16[16,1792]{1,0:T(8,128)(2,1)S(1)} %chip_sum.3), channel_id=1, source_target_pairs={{0,24},{8,16},{16,8},{24,0},{1,25},{9,17},{17,9},{25,1},{2,26},{10... | collective-permute-start | bytes 172040 | tf_op jit(solution)/shard_map/ppermute | solution.py:27
  87.8 4.2 %collective-permute-start.17 = (bf16[16,1792]{1,0:T(8,128)(2,1)S(1)}, bf16[16,1792]{1,0:T(8,128)(2,1)S(1)}, u32[]{:S(2)}, u32[]{:S(2)}) collective-permute-start(bf16[16,1792]{1,0:T(8,128)(2,1)S(1)} %get-tuple-element.47), channel_id=1, source_target_pairs={{0,8},{8,0},{16,24},{24,16},{1,9},{9,1},{17,25},{25,17},{2,10},{10... | collective-permute-start | bytes 172040 | tf_op jit(solution)/shard_map/ppermute | solution.py:27
  87.9 5.1 %collective-permute-start.18 = (bf16[16,1792]{1,0:T(8,128)(2,1)S(1)}, bf16[16,1792]{1,0:T(8,128)(2,1)S(1)}, u32[]{:S(2)}, u32[]{:S(2)}) collective-permute-start(bf16[16,1792]{1,0:T(8,128)(2,1)S(1)} %get-tuple-element.48), channel_id=1, source_target_pairs={{0,16},{8,24},{16,0},{24,8},{1,17},{9,25},{17,1},{25,9},{2,18},{10... | collective-permute-start | bytes 172040 | tf_op jit(solution)/shard_map/ppermute | solution.py:27

commit v2 on v1

--- a/solution.py
+++ b/solution.py
@@ -549,8 +549,9 @@
     pos = query_pos.reshape(1, rows)
     last = row_devices - 1
     tiles = all_tiles(row_devices * PANEL)
-    first_tiles = [t for t in tiles if t[0] != last]
-    last_tiles = [t for t in tiles if t[0] == last]
+    early_panels = (0, 1)
+    first_tiles = [t for t in tiles if t[0] in early_panels]
+    last_tiles = [t for t in tiles if t[0] not in early_panels]
     arrays_of = lambda some: [others[k] if other else halves[k] for k, other in some]
     early = early_attention(
         first_tiles, rows // 2, panel_block, pos, query_latent, q_rope, assemble(arrays_of(first_tiles))

time: 94 us -> 97 us (1.032)
  waiting for transfers between devices: 30.2 us -> 33.6 us
  Pallas kernels: 30.5 us -> 29.5 us
    ppermute x27, waiting for transfers between devices: 30.2 us -> 33.6 us  [swap(): return lax.ppermute(x, axis, [(i, i ^ mask) for i in range(count)])]
    pallas_call x1, Pallas kernels: 3.53 us -> 2.29 us  [early_attention(): pl.pallas_call(functools.partial(early_kernel, tiles, rows), in_specs=[pl...]
  transfers between devices with their start and end apart: 27 -> 27, of which waited for: 10 -> 11; matrix products, arithmetic and copies ran while one was open for 0% -> 0% of each run, Pallas kernels for 31% -> 29%
where the time goes in v2:
time: 97 us; the launch traced here: 96.7 us
  waiting for transfers between devices  33.6 us (35%)
  starting transfers between devices  32.6 us (34%)
  Pallas kernels  29.5 us (30%)
    ppermute x27, waiting for transfers between devices, swap(): return lax.ppermute(x, axis, [(i, i ^ mask) for i in range(count)])  33.6 us
    ppermute x27, starting transfers between devices, swap(): return lax.ppermute(x, axis, [(i, i ^ mask) for i in range(count)])  32.6 us
    pallas_call x2, Pallas kernels, attention(): pl.pallas_call(kernel, in_specs=[pl.BlockSpec(memory_space=pltpu.SMEM)] +...  9.11 us
    pallas_call x3, Pallas kernels, project(): pl.pallas_call(functools.partial(project_kernel, sub, len(parts), len(blo...  7.3 us
    pallas_call x1, Pallas kernels, late_attention(): pl.pallas_call(functools.partial(late_kernel, tiles, rows), in_specs=[pl....  3.5 us
    pallas_call x2, Pallas kernels, load(): pl.pallas_call(load_kernel, in_specs=[pl.BlockSpec(memory_space=pltpu.HBM...  3.26 us
    pallas_call x1, Pallas kernels, early_attention(): pl.pallas_call(functools.partial(early_kernel, tiles, rows), in_specs=[pl...  2.29 us
  transfers between devices with their start and end apart: 27, of which 11 were waited for; matrix products, arithmetic and copies ran while one was open for 0% of the time, Pallas kernels for 29%

profile of v2, /device:TPU:0, one launch (start us, length us, event | category | flops | bytes accessed | tf_op | source)
XLA Modules:
  0.0 96.7 jit_solution(12441947456058024139)
XLA Ops:
  0.0 0.9 panel_half.1.refs_0_
  0.9 4.1 %collective-permute-start.3 = (bf16[576,128]{1,0:T(8,128)(2,1)S(1)}, bf16[576,128]{1,0:T(8,128)(2,1)S(1)}, u32[]{:S(2)}, u32[]{:S(2)}) collective-permute-start(bf16[576,128]{1,0:T(8,128)(2,1)S(1)} %panel_half.1.refs_0_), channel_id=1, source_target_pairs={{0,16},{8,24},{16,0},{24,8},{1,17},{9,25},{17,1},{25,9},{2,18},{10... | collective-permute-start | bytes 442376 | tf_op jit(solution)/shard_map/ppermute | solution.py:27
  5.1 1.6 %collective-permute-start = (bf16[576,128]{1,0:T(8,128)(2,1)S(1)}, bf16[576,128]{1,0:T(8,128)(2,1)S(1)}, u32[]{:S(2)}, u32[]{:S(2)}) collective-permute-start(bf16[576,128]{1,0:T(8,128)(2,1)S(1)} %panel_half.1.refs_0_), channel_id=1, source_target_pairs={{0,8},{8,0},{16,24},{24,16},{1,9},{9,1},{17,25},{25,17},{2,10},{10... | collective-permute-start | bytes 442376 | tf_op jit(solution)/shard_map/ppermute | solution.py:27
  6.6 5.5 %collective-permute-done.3.rest_0_.refs_2_ = bf16[576,128]{1,0:T(8,128)(2,1)S(1)} collective-permute-done((bf16[576,128]{1,0:T(8,128)(2,1)S(1)}, bf16[576,128]{1,0:T(8,128)(2,1)S(1)}, u32[]{:S(2)}, u32[]{:S(2)}) %collective-permute-start.3) | collective-permute-done | bytes 147488 | tf_op jit(solution)/shard_map/ppermute | solution.py:27
  12.2 0.6 collective-permute-start.4
  12.8 0.5 collective-permute-start.2
  13.3 0.0 collective-permute-start.5
  13.3 4.0 %collective-permute-done.4.rest_1_.refs_3_ = bf16[576,128]{1,0:T(8,128)(2,1)S(1)} collective-permute-done((bf16[576,128]{1,0:T(8,128)(2,1)S(1)}, bf16[576,128]{1,0:T(8,128)(2,1)S(1)}, u32[]{:S(2)}, u32[]{:S(2)}) %collective-permute-start.4) | collective-permute-done | bytes 147488 | tf_op jit(solution)/shard_map/ppermute | solution.py:27
  17.3 0.7 copy-done.2
  18.0 1.0 %pack.1 = bf16[64,3200]{1,0:T(8,128)(2,1)S(1)} custom-call(s32[1,128]{1,0:T(1,128)S(1)} %bitcast.1, bf16[128,2048]{1,0:T(8,128)(2,1)} %nope_ref.3, bf16[128,1024]{1,0:T(8,128)(2,1)} %rope_ref.9), custom_call_target="tpu_custom_call" | custom-call | flops 1000000 | bytes 409600 | tf_op jit(solution)/shard_map/pack/pallas_call | solution.py:154
  19.0 1.3 %collective-permute-start.8 = (bf16[64,3200]{1,0:T(8,128)(2,1)S(1)}, bf16[64,3200]{1,0:T(8,128)(2,1)S(1)}, u32[]{:S(2)}, u32[]{:S(2)}) collective-permute-start(bf16[64,3200]{1,0:T(8,128)(2,1)S(1)} %pack.1), channel_id=1, source_target_pairs={{0,8},{8,0},{16,24},{24,16},{1,9},{9,1},{17,25},{25,17},{2,10},{10... | collective-permute-start | bytes 1228808 | tf_op jit(solution)/shard_map/ppermute | solution.py:27
  20.3 1.6 %load.3.rest_4_.up_ref = bf16[16,512,128]{2,1,0:T(8,128)(2,1)S(1)} custom-call(bf16[16,512,128]{2,1,0:T(8,128)(2,1)} %hbm_ref.3), custom_call_target="tpu_custom_call" | custom-call | flops 4000000 | bytes 2097152 | tf_op jit(solution)/shard_map/load/pallas_call | solution.py:81
  21.9 0.0 copy-start.1
  21.9 1.7 %load.2.absorb_ref = bf16[16,128,512]{2,1,0:T(8,128)(2,1)S(1)} custom-call(bf16[16,128,512]{2,1,0:T(8,128)(2,1)} %hbm_ref.2), custom_call_target="tpu_custom_call" | custom-call | flops 4000000 | bytes 2097152 | tf_op jit(solution)/shard_map/load/pallas_call | solution.py:81
  23.6 0.0 copy-start
  23.6 0.0 copy-start.3
  23.6 0.7 queries.1.latent_ref
  24.3 0.0 collective-permute-done.2.refs_3_.refs_5_
  24.3 0.1 assemble.2.keys_ref
  24.5 0.1 copy-done
  24.5 2.3 %early_attention.1 = (f32[1024,1]{1,0:T(8,128)S(1)}, f32[1024,1]{1,0:T(8,128)S(1)}, f32[1024,512]{1,0:T(8,128)S(1)}) custom-call(s32[4]{0:T(128)S(1)} %copy-done.3, s32[1,128]{1,0:T(1,128)S(1)} %bitcast.2, bf16[16,128,512]{2,1,0:T(8,128)(2,1)S(1)} %queries.1.latent_ref, bf16[128,1024]{1,0:T(8,128)(2,1)S(1)} %copy-done, bf16[576,512]{1,0:T(8,128)(2,1)S(1)} %assemble.2.keys_ref), custom_call_target="tpu_custom_call" | custom-call | flops 1140850688 | bytes 4194304 | tf_op jit(solution)/shard_map/early_attention/pallas_call | solution.py:307
  26.9 0.0 collective-permute-done.6.rest_3_.refs_7_
  26.9 3.5 %late_attention.1.refs_0_ = bf16[64,2048]{1,0:T(8,128)(2,1)S(1)} custom-call(s32[4]{0:T(128)S(1)} %copy-done.3, s32[1,128]{1,0:T(1,128)S(1)} %bitcast.3, bf16[16,128,512]{2,1,0:T(8,128)(2,1)S(1)} %queries.1.latent_ref, bf16[128,1024]{1,0:T(8,128)(2,1)S(1)} %copy-done, f32[1024,1]{1,0:T(8,128)S(1)} %get-tuple-element.30.top_ref, ...), custom_call_target="tpu_custom_call" | custom-call | flops 1275068416 | bytes 4194304 | tf_op jit(solution)/shard_map/late_attention/pallas_call | solution.py:327
  30.4 3.4 %collective-permute-start.9 = (bf16[64,2048]{1,0:T(8,128)(2,1)S(1)}, bf16[64,2048]{1,0:T(8,128)(2,1)S(1)}, u32[]{:S(2)}, u32[]{:S(2)}) collective-permute-start(bf16[64,2048]{1,0:T(8,128)(2,1)S(1)} %late_attention.1.refs_0_), channel_id=1, source_target_pairs={{0,16},{8,24},{16,0},{24,8},{1,17},{9,25},{17,1},{25,9},{2,18},{10... | collective-permute-start | bytes 786440 | tf_op jit(solution)/shard_map/ppermute | solution.py:27
  33.8 0.3 collective-permute-start.7
  34.1 0.3 assemble.3.keys_ref
  34.4 4.4 %attention.2 = (bf16[32,2048]{1,0:T(8,128)(2,1)S(1)}, bf16[32,2048]{1,0:T(8,128)(2,1)S(1)}, bf16[1792,2048]{1,0:T(8,128)(2,1)S(1)}) custom-call(s32[4]{0:T(128)S(1)} %copy-done.3, s32[1,128]{1,0:T(1,128)S(1)} %bitcast.4, bf16[16,128,512]{2,1,0:T(8,128)(2,1)S(1)} %queries.1.latent_ref, bf16[128,1024]{1,0:T(8,128)(2,1)S(1)} %copy-done, ...), custom_call_target="tpu_custom_call" | custom-call | flops 2415919104 | bytes 8388608 | tf_op jit(solution)/shard_map/attention/pallas_call | solution.py:391
  38.9 0.2 collective-permute-start.10
  39.0 2.8 %collective-permute-start.11 = (bf16[32,2048]{1,0:T(8,128)(2,1)S(1)}, bf16[32,2048]{1,0:T(8,128)(2,1)S(1)}, u32[]{:S(2)}, u32[]{:S(2)}) collective-permute-start(bf16[32,2048]{1,0:T(8,128)(2,1)S(1)} %get-tuple-element.34.refs_2_), channel_id=1, source_target_pairs={{0,16},{8,24},{16,0},{24,8},{1,17},{9,25},{17,1},{25,9},{2,18},{10... | collective-permute-start | bytes 393224 | tf_op jit(solution)/shard_map/ppermute | solution.py:27
  41.8 0.0 collective-permute-done.8.packed_ref
  41.8 4.7 %attention.3 = (bf16[32,2048]{1,0:T(8,128)(2,1)S(1)}, bf16[32,2048]{1,0:T(8,128)(2,1)S(1)}) custom-call(s32[4]{0:T(128)S(1)} %copy-done.3, bf16[64,3200]{1,0:T(8,128)(2,1)S(1)} %collective-permute-done.8.packed_ref, bf16[16,128,512]{2,1,0:T(8,128)(2,1)S(1)} %load.2.absorb_ref, bf16[16,512,128]{2,1,0:T(8,128)(2,1)S(1)} %load.3.rest_4_.up_ref, ...), custom_call_target="tpu_custom_call" | custom-call | flops 2415919104 | bytes 8388608 | tf_op jit(solution)/shard_map/attention/pallas_call | solution.py:391
  46.6 0.0 collective-permute-done.9.refs_3_
  46.6 1.8 %collective-permute-start.19 = (bf16[64,2048]{1,0:T(8,128)(2,1)S(1)}, bf16[64,2048]{1,0:T(8,128)(2,1)S(1)}, u32[]{:S(2)}, u32[]{:S(2)}) collective-permute-start(bf16[64,2048]{1,0:T(8,128)(2,1)S(1)} %collective-permute-done.9.refs_3_), channel_id=1, source_target_pairs={{0,8},{8,0},{16,24},{24,16},{1,9},{9,1},{17,25},{25,17},{2,10},{10... | collective-permute-start | bytes 786440 | tf_op jit(solution)/shard_map/ppermute | solution.py:27
  48.4 6.1 %collective-permute-done.10.refs_4_ = bf16[32,2048]{1,0:T(8,128)(2,1)S(1)} collective-permute-done((bf16[32,2048]{1,0:T(8,128)(2,1)S(1)}, bf16[32,2048]{1,0:T(8,128)(2,1)S(1)}, u32[]{:S(2)}, u32[]{:S(2)}) %collective-permute-start.10) | collective-permute-done | bytes 131104 | tf_op jit(solution)/shard_map/ppermute | solution.py:27
  54.5 2.8 %collective-permute-done.11.refs_5_ = bf16[32,2048]{1,0:T(8,128)(2,1)S(1)} collective-permute-done((bf16[32,2048]{1,0:T(8,128)(2,1)S(1)}, bf16[32,2048]{1,0:T(8,128)(2,1)S(1)}, u32[]{:S(2)}, u32[]{:S(2)}) %collective-permute-start.11) | collective-permute-done | bytes 131104 | tf_op jit(solution)/shard_map/ppermute | solution.py:27
  57.3 2.3 %project.4 = (bf16[2,4,16,1792]{3,2,1,0:T(8,128)(2,1)S(1)}, f32[2,4,16,1792]{3,2,1,0:T(8,128)S(1)}) custom-call(bf16[64,2048]{1,0:T(8,128)(2,1)S(1)} %collective-permute-done.7.refs_0_, bf16[32,2048]{1,0:T(8,128)(2,1)S(1)} %get-tuple-element.37.refs_1_, bf16[32,2048]{1,0:T(8,128)(2,1)S(1)} %get-tuple-element.38.refs_2_, ...), custom_call_target="tpu_custom_call" | custom-call | flops 1879048192 | bytes 7864320 | tf_op jit(solution)/shard_map/project/pallas_call | solution.py:429
  59.6 0.1 collective-permute-start.13
  59.7 0.1 collective-permute-start.20
  59.7 2.0 %collective-permute-start.21 = (bf16[32,2048]{1,0:T(8,128)(2,1)S(1)}, bf16[32,2048]{1,0:T(8,128)(2,1)S(1)}, u32[]{:S(2)}, u32[]{:S(2)}) collective-permute-start(bf16[32,2048]{1,0:T(8,128)(2,1)S(1)} %collective-permute-done.11.refs_5_), channel_id=1, source_target_pairs={{0,8},{8,0},{16,24},{24,16},{1,9},{9,1},{17,25},{25,17},{2,10},{10... | collective-permute-start | bytes 393224 | tf_op jit(solution)/shard_map/ppermute | solution.py:27
  61.7 2.5 %project.3 = (bf16[1,4,16,1792]{3,2,1,0:T(8,128)(2,1)S(1)}, f32[1,4,16,1792]{3,2,1,0:T(8,128)S(1)}) custom-call(bf16[64,2048]{1,0:T(8,128)(2,1)S(1)} %late_attention.1.refs_0_, bf16[32,2048]{1,0:T(8,128)(2,1)S(1)} %get-tuple-element.33.refs_1_, bf16[32,2048]{1,0:T(8,128)(2,1)S(1)} %get-tuple-element.34.refs_2_, ...), custom_call_target="tpu_custom_call" | custom-call | flops 939524096 | bytes 7864320 | tf_op jit(solution)/shard_map/project/pallas_call | solution.py:429
  64.3 0.1 collective-permute-start.12
  64.3 1.8 %collective-permute-done.20.refs_1_ = bf16[32,2048]{1,0:T(8,128)(2,1)S(1)} collective-permute-done((bf16[32,2048]{1,0:T(8,128)(2,1)S(1)}, bf16[32,2048]{1,0:T(8,128)(2,1)S(1)}, u32[]{:S(2)}, u32[]{:S(2)}) %collective-permute-start.20) | collective-permute-done | bytes 131104 | tf_op jit(solution)/shard_map/ppermute | solution.py:27
  66.1 2.3 %collective-permute-done.21.refs_2_ = bf16[32,2048]{1,0:T(8,128)(2,1)S(1)} collective-permute-done((bf16[32,2048]{1,0:T(8,128)(2,1)S(1)}, bf16[32,2048]{1,0:T(8,128)(2,1)S(1)}, u32[]{:S(2)}, u32[]{:S(2)}) %collective-permute-start.21) | collective-permute-done | bytes 131104 | tf_op jit(solution)/shard_map/ppermute | solution.py:27
  68.4 0.0 collective-permute-done.19.refs_0_
  68.4 2.5 %project.5 = (bf16[1,4,16,1792]{3,2,1,0:T(8,128)(2,1)S(1)}, f32[1,4,16,1792]{3,2,1,0:T(8,128)S(1)}) custom-call(bf16[64,2048]{1,0:T(8,128)(2,1)S(1)} %collective-permute-done.19.refs_0_, bf16[32,2048]{1,0:T(8,128)(2,1)S(1)} %collective-permute-done.20.refs_1_, bf16[32,2048]{1,0:T(8,128)(2,1)S(1)} %collective-permute-done.21.refs_2_, ...), custom_call_target="tpu_custom_call" | custom-call | flops 939524096 | bytes 7864320 | tf_op jit(solution)/shard_map/project/pallas_call | solution.py:429
  70.9 0.1 collective-permute-start.22
  70.9 0.0 collective-permute-done.12.refs_2_
  71.0 0.1 pair_sum.2
  71.1 1.6 %collective-permute-start.14 = (bf16[3,16,1792]{2,1,0:T(8,128)(2,1)S(1)}, bf16[3,16,1792]{2,1,0:T(8,128)(2,1)S(1)}, u32[]{:S(2)}, u32[]{:S(2)}) collective-permute-start(bf16[3,16,1792]{2,1,0:T(8,128)(2,1)S(1)} %get-tuple-element.43), channel_id=1, source_target_pairs={{0,2},{1,3},{2,0},{3,1},{4,6},{5,7},{6,4},{7,5},{8,10},{9,11},{10,... | collective-permute-start | bytes 516104 | tf_op jit(solution)/shard_map/ppermute | solution.py:27
  72.7 1.5 %collective-permute-start.15 = (bf16[3,16,1792]{2,1,0:T(8,128)(2,1)S(1)}, bf16[3,16,1792]{2,1,0:T(8,128)(2,1)S(1)}, u32[]{:S(2)}, u32[]{:S(2)}) collective-permute-start(bf16[3,16,1792]{2,1,0:T(8,128)(2,1)S(1)} %get-tuple-element.44), channel_id=1, source_target_pairs={{0,4},{1,5},{2,6},{3,7},{4,0},{5,1},{6,2},{7,3},{8,12},{9,13},{10,... | collective-permute-start | bytes 516104 | tf_op jit(solution)/shard_map/ppermute | solution.py:27
  74.2 0.5 collective-permute-start.16
  74.7 1.6 %collective-permute-start.23 = (bf16[1,16,1792]{2,1,0:T(8,128)(2,1)S(1)}, bf16[1,16,1792]{2,1,0:T(8,128)(2,1)S(1)}, u32[]{:S(2)}, u32[]{:S(2)}) collective-permute-start(bf16[1,16,1792]{2,1,0:T(8,128)(2,1)S(1)} %get-tuple-element.52), channel_id=1, source_target_pairs={{0,2},{1,3},{2,0},{3,1},{4,6},{5,7},{6,4},{7,5},{8,10},{9,11},{10,... | collective-permute-start | bytes 172040 | tf_op jit(solution)/shard_map/ppermute | solution.py:27
  76.3 1.5 %collective-permute-start.24 = (bf16[1,16,1792]{2,1,0:T(8,128)(2,1)S(1)}, bf16[1,16,1792]{2,1,0:T(8,128)(2,1)S(1)}, u32[]{:S(2)}, u32[]{:S(2)}) collective-permute-start(bf16[1,16,1792]{2,1,0:T(8,128)(2,1)S(1)} %get-tuple-element.53), channel_id=1, source_target_pairs={{0,4},{1,5},{2,6},{3,7},{4,0},{5,1},{6,2},{7,3},{8,12},{9,13},{10,... | collective-permute-start | bytes 172040 | tf_op jit(solution)/shard_map/ppermute | solution.py:27
  77.8 5.1 %collective-permute-done.23.refs_1_ = bf16[1,16,1792]{2,1,0:T(8,128)(2,1)S(1)} collective-permute-done((bf16[1,16,1792]{2,1,0:T(8,128)(2,1)S(1)}, bf16[1,16,1792]{2,1,0:T(8,128)(2,1)S(1)}, u32[]{:S(2)}, u32[]{:S(2)}) %collective-permute-start.23) | collective-permute-done | bytes 57376 | tf_op jit(solution)/shard_map/ppermute | solution.py:27
  82.9 2.4 %collective-permute-start.25 = (bf16[1,16,1792]{2,1,0:T(8,128)(2,1)S(1)}, bf16[1,16,1792]{2,1,0:T(8,128)(2,1)S(1)}, u32[]{:S(2)}, u32[]{:S(2)}) collective-permute-start(bf16[1,16,1792]{2,1,0:T(8,128)(2,1)S(1)} %get-tuple-element.54), channel_id=1, source_target_pairs={{0,6},{1,7},{2,4},{3,5},{4,2},{5,3},{6,0},{7,1},{8,14},{9,15},{10,... | collective-permute-start | bytes 172040 | tf_op jit(solution)/shard_map/ppermute | solution.py:27
  85.3 2.6 %collective-permute-done.25.refs_3_ = bf16[1,16,1792]{2,1,0:T(8,128)(2,1)S(1)} collective-permute-done((bf16[1,16,1792]{2,1,0:T(8,128)(2,1)S(1)}, bf16[1,16,1792]{2,1,0:T(8,128)(2,1)S(1)}, u32[]{:S(2)}, u32[]{:S(2)}) %collective-permute-start.25) | collective-permute-done | bytes 57376 | tf_op jit(solution)/shard_map/ppermute | solution.py:27
  88.0 2.7 %collective-permute-start.26 = (bf16[16,1792]{1,0:T(8,128)(2,1)S(1)}, bf16[16,1792]{1,0:T(8,128)(2,1)S(1)}, u32[]{:S(2)}, u32[]{:S(2)}) collective-permute-start(bf16[16,1792]{1,0:T(8,128)(2,1)S(1)} %chip_sum.3), channel_id=1, source_target_pairs={{0,24},{8,16},{16,8},{24,0},{1,25},{9,17},{17,9},{25,1},{2,26},{10... | collective-permute-start | bytes 172040 | tf_op jit(solution)/shard_map/ppermute | solution.py:27
  90.7 0.1 chip_sum.2
  90.8 0.1 collective-permute-start.17
  90.9 1.7 %collective-permute-start.18 = (bf16[16,1792]{1,0:T(8,128)(2,1)S(1)}, bf16[16,1792]{1,0:T(8,128)(2,1)S(1)}, u32[]{:S(2)}, u32[]{:S(2)}) collective-permute-start(bf16[16,1792]{1,0:T(8,128)(2,1)S(1)} %get-tuple-element.48), channel_id=1, source_target_pairs={{0,16},{8,24},{16,0},{24,8},{1,17},{9,25},{17,1},{25,9},{2,18},{10... | collective-permute-start | bytes 172040 | tf_op jit(solution)/shard_map/ppermute | solution.py:27
  92.6 1.7 %collective-permute-done.26.refs_3_ = bf16[16,1792]{1,0:T(8,128)(2,1)S(1)} collective-permute-done((bf16[16,1792]{1,0:T(8,128)(2,1)S(1)}, bf16[16,1792]{1,0:T(8,128)(2,1)S(1)}, u32[]{:S(2)}, u32[]{:S(2)}) %collective-permute-start.26) | collective-permute-done | bytes 57376 | tf_op jit(solution)/shard_map/ppermute | solution.py:27
  94.4 0.7 collective-permute-done.17.refs_1_
  95.0 1.0 %collective-permute-done.18.refs_2_ = bf16[16,1792]{1,0:T(8,128)(2,1)S(1)} collective-permute-done((bf16[16,1792]{1,0:T(8,128)(2,1)S(1)}, bf16[16,1792]{1,0:T(8,128)(2,1)S(1)}, u32[]{:S(2)}, u32[]{:S(2)}) %collective-permute-start.18) | collective-permute-done | bytes 57376 | tf_op jit(solution)/shard_map/ppermute | solution.py:27
  96.0 0.7 finish.1
  (17 shorter events, 0.1 us)
Async XLA Ops:
  0.9 11.2 %collective-permute-start.3 = (bf16[576,128]{1,0:T(8,128)(2,1)S(1)}, bf16[576,128]{1,0:T(8,128)(2,1)S(1)}, u32[]{:S(2)}, u32[]{:S(2)}) collective-permute-start(bf16[576,128]{1,0:T(8,128)(2,1)S(1)} %panel_half.1.refs_0_), channel_id=1, source_target_pairs={{0,16},{8,24},{16,0},{24,8},{1,17},{9,25},{17,1},{25,9},{2,18},{10... | collective-permute-start | bytes 442376 | tf_op jit(solution)/shard_map/ppermute | solution.py:27
  5.1 7.7 %collective-permute-start = (bf16[576,128]{1,0:T(8,128)(2,1)S(1)}, bf16[576,128]{1,0:T(8,128)(2,1)S(1)}, u32[]{:S(2)}, u32[]{:S(2)}) collective-permute-start(bf16[576,128]{1,0:T(8,128)(2,1)S(1)} %panel_half.1.refs_0_), channel_id=1, source_target_pairs={{0,8},{8,0},{16,24},{24,16},{1,9},{9,1},{17,25},{25,17},{2,10},{10... | collective-permute-start | bytes 442376 | tf_op jit(solution)/shard_map/ppermute | solution.py:27
  12.2 5.1 %collective-permute-start.4 = (bf16[576,128]{1,0:T(8,128)(2,1)S(1)}, bf16[576,128]{1,0:T(8,128)(2,1)S(1)}, u32[]{:S(2)}, u32[]{:S(2)}) collective-permute-start(bf16[576,128]{1,0:T(8,128)(2,1)S(1)} %collective-permute-done.3.rest_0_.refs_2_), channel_id=1, source_target_pairs={{0,8},{8,0},{16,24},{24,16},{1,9},{9,1},{17,25},{25,17},{2,10},{10... | collective-permute-start | bytes 442376 | tf_op jit(solution)/shard_map/ppermute | solution.py:27
  12.8 11.5 %collective-permute-start.1 = (bf16[576,128]{1,0:T(8,128)(2,1)S(1)}, bf16[576,128]{1,0:T(8,128)(2,1)S(1)}, u32[]{:S(2)}, u32[]{:S(2)}) collective-permute-start(bf16[576,128]{1,0:T(8,128)(2,1)S(1)} %panel_half.1.refs_0_), channel_id=1, source_target_pairs={{0,1},{1,0},{2,3},{3,2},{4,5},{5,4},{6,7},{7,6},{8,9},{9,8},{10,11... | collective-permute-start | bytes 442376 | tf_op jit(solution)/shard_map/ppermute | solution.py:27
  12.8 11.5 %collective-permute-start.2 = (bf16[576,128]{1,0:T(8,128)(2,1)S(1)}, bf16[576,128]{1,0:T(8,128)(2,1)S(1)}, u32[]{:S(2)}, u32[]{:S(2)}) collective-permute-start(bf16[576,128]{1,0:T(8,128)(2,1)S(1)} %collective-permute-done.refs_1_), channel_id=1, source_target_pairs={{0,1},{1,0},{2,3},{3,2},{4,5},{5,4},{6,7},{7,6},{8,9},{9,8},{10,11... | collective-permute-start | bytes 442376 | tf_op jit(solution)/shard_map/ppermute | solution.py:27
  13.3 13.5 %collective-permute-start.5 = (bf16[576,128]{1,0:T(8,128)(2,1)S(1)}, bf16[576,128]{1,0:T(8,128)(2,1)S(1)}, u32[]{:S(2)}, u32[]{:S(2)}) collective-permute-start(bf16[576,128]{1,0:T(8,128)(2,1)S(1)} %collective-permute-done.3.rest_0_.refs_2_), channel_id=1, source_target_pairs={{0,1},{1,0},{2,3},{3,2},{4,5},{5,4},{6,7},{7,6},{8,9},{9,8},{10,11... | collective-permute-start | bytes 442376 | tf_op jit(solution)/shard_map/ppermute | solution.py:27
  17.3 9.5 %collective-permute-start.6 = (bf16[576,128]{1,0:T(8,128)(2,1)S(1)}, bf16[576,128]{1,0:T(8,128)(2,1)S(1)}, u32[]{:S(2)}, u32[]{:S(2)}) collective-permute-start(bf16[576,128]{1,0:T(8,128)(2,1)S(1)} %collective-permute-done.4.rest_1_.refs_3_), channel_id=1, source_target_pairs={{0,1},{1,0},{2,3},{3,2},{4,5},{5,4},{6,7},{7,6},{8,9},{9,8},{10,11... | collective-permute-start | bytes 442376 | tf_op jit(solution)/shard_map/ppermute | solution.py:27
  17.3 0.7 copy-start.2
  19.0 22.9 %collective-permute-start.8 = (bf16[64,3200]{1,0:T(8,128)(2,1)S(1)}, bf16[64,3200]{1,0:T(8,128)(2,1)S(1)}, u32[]{:S(2)}, u32[]{:S(2)}) collective-permute-start(bf16[64,3200]{1,0:T(8,128)(2,1)S(1)} %pack.1), channel_id=1, source_target_pairs={{0,8},{8,0},{16,24},{24,16},{1,9},{9,1},{17,25},{25,17},{2,10},{10... | collective-permute-start | bytes 1228808 | tf_op jit(solution)/shard_map/ppermute | solution.py:27
  21.9 1.7 %copy-start.1 = (bf16[128,2048]{1,0:T(8,128)(2,1)S(1)}, bf16[128,2048]{1,0:T(8,128)(2,1)}, u32[]{:S(2)}) copy-start(bf16[128,2048]{1,0:T(8,128)(2,1)} %nope_ref.3) | copy-start | bytes 1572868
  23.6 1.0 copy-start
  23.6 0.9 copy-start.3
  30.4 16.2 %collective-permute-start.9 = (bf16[64,2048]{1,0:T(8,128)(2,1)S(1)}, bf16[64,2048]{1,0:T(8,128)(2,1)S(1)}, u32[]{:S(2)}, u32[]{:S(2)}) collective-permute-start(bf16[64,2048]{1,0:T(8,128)(2,1)S(1)} %late_attention.1.refs_0_), channel_id=1, source_target_pairs={{0,16},{8,24},{16,0},{24,8},{1,17},{9,25},{17,1},{25,9},{2,18},{10... | collective-permute-start | bytes 786440 | tf_op jit(solution)/shard_map/ppermute | solution.py:27
  33.8 23.4 %collective-permute-start.7 = (bf16[64,2048]{1,0:T(8,128)(2,1)S(1)}, bf16[64,2048]{1,0:T(8,128)(2,1)S(1)}, u32[]{:S(2)}, u32[]{:S(2)}) collective-permute-start(bf16[64,2048]{1,0:T(8,128)(2,1)S(1)} %late_attention.1.refs_0_), channel_id=1, source_target_pairs={{0,8},{8,0},{16,24},{24,16},{1,9},{9,1},{17,25},{25,17},{2,10},{10... | collective-permute-start | bytes 786440 | tf_op jit(solution)/shard_map/ppermute | solution.py:27
  38.9 15.6 %collective-permute-start.10 = (bf16[32,2048]{1,0:T(8,128)(2,1)S(1)}, bf16[32,2048]{1,0:T(8,128)(2,1)S(1)}, u32[]{:S(2)}, u32[]{:S(2)}) collective-permute-start(bf16[32,2048]{1,0:T(8,128)(2,1)S(1)} %get-tuple-element.33.refs_1_), channel_id=1, source_target_pairs={{0,16},{8,24},{16,0},{24,8},{1,17},{9,25},{17,1},{25,9},{2,18},{10... | collective-permute-start | bytes 393224 | tf_op jit(solution)/shard_map/ppermute | solution.py:27
  39.0 18.2 %collective-permute-start.11 = (bf16[32,2048]{1,0:T(8,128)(2,1)S(1)}, bf16[32,2048]{1,0:T(8,128)(2,1)S(1)}, u32[]{:S(2)}, u32[]{:S(2)}) collective-permute-start(bf16[32,2048]{1,0:T(8,128)(2,1)S(1)} %get-tuple-element.34.refs_2_), channel_id=1, source_target_pairs={{0,16},{8,24},{16,0},{24,8},{1,17},{9,25},{17,1},{25,9},{2,18},{10... | collective-permute-start | bytes 393224 | tf_op jit(solution)/shard_map/ppermute | solution.py:27
  46.6 21.8 %collective-permute-start.19 = (bf16[64,2048]{1,0:T(8,128)(2,1)S(1)}, bf16[64,2048]{1,0:T(8,128)(2,1)S(1)}, u32[]{:S(2)}, u32[]{:S(2)}) collective-permute-start(bf16[64,2048]{1,0:T(8,128)(2,1)S(1)} %collective-permute-done.9.refs_3_), channel_id=1, source_target_pairs={{0,8},{8,0},{16,24},{24,16},{1,9},{9,1},{17,25},{25,17},{2,10},{10... | collective-permute-start | bytes 786440 | tf_op jit(solution)/shard_map/ppermute | solution.py:27
  59.6 11.4 %collective-permute-start.13 = (bf16[2,4,16,1792]{3,2,1,0:T(8,128)(2,1)S(1)}, bf16[2,4,16,1792]{3,2,1,0:T(8,128)(2,1)S(1)}, u32[]{:S(2)}, u32[]{:S(2)}) collective-permute-start(bf16[2,4,16,1792]{3,2,1,0:T(8,128)(2,1)S(1)} %get-tuple-element.41), channel_id=1, source_target_pairs={{0,1},{1,0},{2,3},{3,2},{4,5},{5,4},{6,7},{7,6},{8,9},{9,8},{10,11... | collective-permute-start | bytes 1376264 | tf_op jit(solution)/shard_map/ppermute | solution.py:27
  59.7 6.4 %collective-permute-start.20 = (bf16[32,2048]{1,0:T(8,128)(2,1)S(1)}, bf16[32,2048]{1,0:T(8,128)(2,1)S(1)}, u32[]{:S(2)}, u32[]{:S(2)}) collective-permute-start(bf16[32,2048]{1,0:T(8,128)(2,1)S(1)} %collective-permute-done.10.refs_4_), channel_id=1, source_target_pairs={{0,8},{8,0},{16,24},{24,16},{1,9},{9,1},{17,25},{25,17},{2,10},{10... | collective-permute-start | bytes 393224 | tf_op jit(solution)/shard_map/ppermute | solution.py:27
  59.7 8.6 %collective-permute-start.21 = (bf16[32,2048]{1,0:T(8,128)(2,1)S(1)}, bf16[32,2048]{1,0:T(8,128)(2,1)S(1)}, u32[]{:S(2)}, u32[]{:S(2)}) collective-permute-start(bf16[32,2048]{1,0:T(8,128)(2,1)S(1)} %collective-permute-done.11.refs_5_), channel_id=1, source_target_pairs={{0,8},{8,0},{16,24},{24,16},{1,9},{9,1},{17,25},{25,17},{2,10},{10... | collective-permute-start | bytes 393224 | tf_op jit(solution)/shard_map/ppermute | solution.py:27
  64.3 6.7 %collective-permute-start.12 = (bf16[1,4,16,1792]{3,2,1,0:T(8,128)(2,1)S(1)}, bf16[1,4,16,1792]{3,2,1,0:T(8,128)(2,1)S(1)}, u32[]{:S(2)}, u32[]{:S(2)}) collective-permute-start(bf16[1,4,16,1792]{3,2,1,0:T(8,128)(2,1)S(1)} %get-tuple-element.40), channel_id=1, source_target_pairs={{0,1},{1,0},{2,3},{3,2},{4,5},{5,4},{6,7},{7,6},{8,9},{9,8},{10,11... | collective-permute-start | bytes 688136 | tf_op jit(solution)/shard_map/ppermute | solution.py:27
  70.9 3.8 %collective-permute-start.22 = (bf16[1,4,16,1792]{3,2,1,0:T(8,128)(2,1)S(1)}, bf16[1,4,16,1792]{3,2,1,0:T(8,128)(2,1)S(1)}, u32[]{:S(2)}, u32[]{:S(2)}) collective-permute-start(bf16[1,4,16,1792]{3,2,1,0:T(8,128)(2,1)S(1)} %get-tuple-element.50), channel_id=1, source_target_pairs={{0,1},{1,0},{2,3},{3,2},{4,5},{5,4},{6,7},{7,6},{8,9},{9,8},{10,11... | collective-permute-start | bytes 688136 | tf_op jit(solution)/shard_map/ppermute | solution.py:27
  71.1 19.6 %collective-permute-start.14 = (bf16[3,16,1792]{2,1,0:T(8,128)(2,1)S(1)}, bf16[3,16,1792]{2,1,0:T(8,128)(2,1)S(1)}, u32[]{:S(2)}, u32[]{:S(2)}) collective-permute-start(bf16[3,16,1792]{2,1,0:T(8,128)(2,1)S(1)} %get-tuple-element.43), channel_id=1, source_target_pairs={{0,2},{1,3},{2,0},{3,1},{4,6},{5,7},{6,4},{7,5},{8,10},{9,11},{10,... | collective-permute-start | bytes 516104 | tf_op jit(solution)/shard_map/ppermute | solution.py:27
  72.7 18.0 %collective-permute-start.15 = (bf16[3,16,1792]{2,1,0:T(8,128)(2,1)S(1)}, bf16[3,16,1792]{2,1,0:T(8,128)(2,1)S(1)}, u32[]{:S(2)}, u32[]{:S(2)}) collective-permute-start(bf16[3,16,1792]{2,1,0:T(8,128)(2,1)S(1)} %get-tuple-element.44), channel_id=1, source_target_pairs={{0,4},{1,5},{2,6},{3,7},{4,0},{5,1},{6,2},{7,3},{8,12},{9,13},{10,... | collective-permute-start | bytes 516104 | tf_op jit(solution)/shard_map/ppermute | solution.py:27
  74.2 16.5 %collective-permute-start.16 = (bf16[3,16,1792]{2,1,0:T(8,128)(2,1)S(1)}, bf16[3,16,1792]{2,1,0:T(8,128)(2,1)S(1)}, u32[]{:S(2)}, u32[]{:S(2)}) collective-permute-start(bf16[3,16,1792]{2,1,0:T(8,128)(2,1)S(1)} %get-tuple-element.45), channel_id=1, source_target_pairs={{0,6},{1,7},{2,4},{3,5},{4,2},{5,3},{6,0},{7,1},{8,14},{9,15},{10,... | collective-permute-start | bytes 516104 | tf_op jit(solution)/shard_map/ppermute | solution.py:27
  74.7 8.2 %collective-permute-start.23 = (bf16[1,16,1792]{2,1,0:T(8,128)(2,1)S(1)}, bf16[1,16,1792]{2,1,0:T(8,128)(2,1)S(1)}, u32[]{:S(2)}, u32[]{:S(2)}) collective-permute-start(bf16[1,16,1792]{2,1,0:T(8,128)(2,1)S(1)} %get-tuple-element.52), channel_id=1, source_target_pairs={{0,2},{1,3},{2,0},{3,1},{4,6},{5,7},{6,4},{7,5},{8,10},{9,11},{10,... | collective-permute-start | bytes 172040 | tf_op jit(solution)/shard_map/ppermute | solution.py:27
  76.3 9.1 %collective-permute-start.24 = (bf16[1,16,1792]{2,1,0:T(8,128)(2,1)S(1)}, bf16[1,16,1792]{2,1,0:T(8,128)(2,1)S(1)}, u32[]{:S(2)}, u32[]{:S(2)}) collective-permute-start(bf16[1,16,1792]{2,1,0:T(8,128)(2,1)S(1)} %get-tuple-element.53), channel_id=1, source_target_pairs={{0,4},{1,5},{2,6},{3,7},{4,0},{5,1},{6,2},{7,3},{8,12},{9,13},{10,... | collective-permute-start | bytes 172040 | tf_op jit(solution)/shard_map/ppermute | solution.py:27
  82.9 5.1 %collective-permute-start.25 = (bf16[1,16,1792]{2,1,0:T(8,128)(2,1)S(1)}, bf16[1,16,1792]{2,1,0:T(8,128)(2,1)S(1)}, u32[]{:S(2)}, u32[]{:S(2)}) collective-permute-start(bf16[1,16,1792]{2,1,0:T(8,128)(2,1)S(1)} %get-tuple-element.54), channel_id=1, source_target_pairs={{0,6},{1,7},{2,4},{3,5},{4,2},{5,3},{6,0},{7,1},{8,14},{9,15},{10,... | collective-permute-start | bytes 172040 | tf_op jit(solution)/shard_map/ppermute | solution.py:27
  88.0 6.4 %collective-permute-start.26 = (bf16[16,1792]{1,0:T(8,128)(2,1)S(1)}, bf16[16,1792]{1,0:T(8,128)(2,1)S(1)}, u32[]{:S(2)}, u32[]{:S(2)}) collective-permute-start(bf16[16,1792]{1,0:T(8,128)(2,1)S(1)} %chip_sum.3), channel_id=1, source_target_pairs={{0,24},{8,16},{16,8},{24,0},{1,25},{9,17},{17,9},{25,1},{2,26},{10... | collective-permute-start | bytes 172040 | tf_op jit(solution)/shard_map/ppermute | solution.py:27
  90.8 4.2 %collective-permute-start.17 = (bf16[16,1792]{1,0:T(8,128)(2,1)S(1)}, bf16[16,1792]{1,0:T(8,128)(2,1)S(1)}, u32[]{:S(2)}, u32[]{:S(2)}) collective-permute-start(bf16[16,1792]{1,0:T(8,128)(2,1)S(1)} %get-tuple-element.47), channel_id=1, source_target_pairs={{0,8},{8,0},{16,24},{24,16},{1,9},{9,1},{17,25},{25,17},{2,10},{10... | collective-permute-start | bytes 172040 | tf_op jit(solution)/shard_map/ppermute | solution.py:27
  90.9 5.1 %collective-permute-start.18 = (bf16[16,1792]{1,0:T(8,128)(2,1)S(1)}, bf16[16,1792]{1,0:T(8,128)(2,1)S(1)}, u32[]{:S(2)}, u32[]{:S(2)}) collective-permute-start(bf16[16,1792]{1,0:T(8,128)(2,1)S(1)} %get-tuple-element.48), channel_id=1, source_target_pairs={{0,16},{8,24},{16,0},{24,8},{1,17},{9,25},{17,1},{25,9},{2,18},{10... | collective-permute-start | bytes 172040 | tf_op jit(solution)/shard_map/ppermute | solution.py:27
